TPU v7x, 128 devices: a whole 4x4x4 slice. The times are simulated.
128 devices in a mesh: rep: 1, dp: 128 (over x, y, z, core).
Axes of the slice: x: 4, y: 4, z: 4, core: 2. Of those that a mesh axis runs over, the one named last changes fastest.
Arguments:
- x: bfloat16 [128, 2048, 896], P(('rep', 'dp'))
- dy: bfloat16 [128, 2048, 896], P(('rep', 'dp'))
- w_gate: bfloat16 [2, 896, 2304], P(None, 'dp')
- w_up: bfloat16 [2, 896, 2304], P(None, 'dp')
- w_down: bfloat16 [2, 2304, 896], P(None, 'dp')
Outputs:
- output 1: bfloat16 [128, 2048, 896], P(('rep', 'dp'))
- output 2: bfloat16 [2, 896, 2304], P('rep', 'dp')
- output 3: bfloat16 [2, 896, 2304], P('rep', 'dp')
- output 4: bfloat16 [2, 2304, 896], P('rep', 'dp')
All inputs are finite; a program needn't handle non-finite values.
Results may differ from a plain program's by a relative error of at most 0.018.
Values are sent between devices in bfloat16 or wider.
A program may use at most 1.5 GiB of HBM per device.

v0:
```python
import jax
import jax.numpy as jnp
from jax import lax

NAMES = ("w_gate", "w_up", "w_down")


def matmul(a, w):
    return jnp.dot(a, w, preferred_element_type=jnp.float32).astype(jnp.bfloat16)


def normed(h):
    wide = h.astype(jnp.float32)
    scale = lax.rsqrt(jnp.mean(wide**2, -1, keepdims=True) + 1e-6)
    return (wide * scale).astype(jnp.bfloat16)


def layer(h, w):
    a = normed(h)
    gate = jnp.dot(a, w["w_gate"], preferred_element_type=jnp.float32)
    up = jnp.dot(a, w["w_up"], preferred_element_type=jnp.float32)
    return h + matmul((jax.nn.silu(gate) * up).astype(jnp.bfloat16), w["w_down"])


def stack(weights, h):
    for number in range(weights["w_gate"].shape[0]):
        h = layer(h, {name: w[number] for name, w in weights.items()})
    return h


def solution(mesh):
    groups = mesh.shape["rep"]

    def step(x, dy, *weights):
        shape = x.shape
        x, dy = (t.reshape(groups, -1, *t.shape[1:]) for t in (x, dy))

        def of_a_group(x, dy):
            _, back = jax.vjp(stack, dict(zip(NAMES, weights, strict=True)), x)
            by_weights, by_x = back(dy)
            return (by_x, *(by_weights[name] for name in NAMES))

        by_x, *by_weights = jax.vmap(of_a_group)(x, dy)
        return (by_x.reshape(shape), *(t.reshape(-1, *t.shape[2:]) for t in by_weights))

    return step
```

profile of v0, /device:TPU:17, one launch (start us, length us, event | category | flops | bytes accessed | tf_op | source)
XLA Modules:
  0.0 1423.4 jit_solution(878963510388579576)
XLA Ops:
  29.9 51.7 %all-gather.29.cloned.1.call-done = bf16[1,896,2304]{2,0,1:T(2,128)(2,1)} async-done(((bf16[1,7,2304]{2,0,1:T(2,128)(2,1)}), bf16[1,896,2304]{2,0,1:T(2,128)(2,1)}) %all-gather.29.cloned.1.call-update) | async-done | bytes 4128784 | tf_op jit(solution)/vmap(jvp())/squeeze | solution.py:27
  81.6 17.8 %fusion.61 = f32[2048,2304]{1,0:T(8,128)} fusion(bf16[1,2048,896]{1,2,0:T(8,128)(2,1)} %copy.21, f32[2048]{0:T(1024)S(1)} %bitcast.245, bf16[1,896,2304]{2,0,1:T(2,128)(2,1)} %all-gather.29.cloned.1.call-done), kind=kOutput, calls=%fused_computation.78 | convolution fusion | flops 8461221888 | bytes 26681344 | tf_op jit(solution)/vmap(jvp())/dot_general | solution.py:20
  99.4 52.9 %all-gather.31.cloned.1.call-done = bf16[1,896,2304]{2,0,1:T(2,128)(2,1)} async-done(((bf16[1,7,2304]{2,0,1:T(2,128)(2,1)}), bf16[1,896,2304]{2,0,1:T(2,128)(2,1)}) %all-gather.31.cloned.1.call-update) | async-done | bytes 4128784 | tf_op jit(solution)/vmap(jvp())/squeeze | solution.py:27
  152.2 18.0 %fusion.57 = f32[2048,2304]{1,0:T(8,128)} fusion(bf16[1,2048,896]{1,2,0:T(8,128)(2,1)} %copy.21, f32[2048]{0:T(1024)S(1)} %bitcast.246, bf16[1,896,2304]{2,0,1:T(2,128)(2,1)} %all-gather.31.cloned.1.call-done), kind=kOutput, calls=%fused_computation.74 | convolution fusion | flops 8461221888 | bytes 26681344 | tf_op jit(solution)/vmap(jvp())/dot_general | solution.py:21
  170.2 14.1 fusion.30
  184.3 38.0 %all-gather.33.cloned.1.call-done = bf16[1,2304,896]{2,0,1:T(2,128)(2,1)} async-done(((bf16[1,18,896]{2,0,1:T(2,128)(2,1)}), bf16[1,2304,896]{2,0,1:T(2,128)(2,1)}) %all-gather.33.cloned.1.call-update) | async-done | bytes 4128784 | tf_op jit(solution)/vmap(jvp())/squeeze | solution.py:27
  222.3 16.1 %fusion.41 = (f32[2048]{0:T(1024)S(1)}, bf16[1,2048,896]{1,2,0:T(8,128)(2,1)}) fusion(bf16[1,2048,896]{1,2,0:T(8,128)(2,1)} %copy.21, bf16[2048,2304]{1,0:T(8,128)(2,1)} %fusion.30, bf16[1,2304,896]{2,0,1:T(2,128)(2,1)} %all-gather.33.cloned.1.call-done), kind=kOutput, calls=%fused_computation.58 | convolution fusion | flops 8464889856 | bytes 20914176 | tf_op jit(solution)/vmap(jvp())/dot_general | solution.py:9
  239.0 53.8 %all-gather.35.cloned.1.call-done = bf16[1,896,2304]{2,0,1:T(2,128)(2,1)} async-done(((bf16[1,7,2304]{2,0,1:T(2,128)(2,1)}), bf16[1,896,2304]{2,0,1:T(2,128)(2,1)}) %all-gather.35.cloned.1.call-update) | async-done | bytes 4128784 | tf_op jit(solution)/vmap(jvp())/squeeze | solution.py:27
  292.8 17.8 %fusion.51 = f32[2048,2304]{1,0:T(8,128)} fusion(bf16[1,2048,896]{1,2,0:T(8,128)(2,1)} %get-tuple-element.89, f32[2048]{0:T(1024)S(1)} %bitcast.250, bf16[1,896,2304]{2,0,1:T(2,128)(2,1)} %all-gather.35.cloned.1.call-done), kind=kOutput, calls=%fused_computation.68 | convolution fusion | flops 8461221888 | bytes 26681344 | tf_op jit(solution)/vmap(jvp())/dot_general | solution.py:20
  310.6 52.1 %all-gather.37.cloned.1.call-done = bf16[1,2304,896]{2,0,1:T(2,128)(2,1)} async-done(((bf16[1,18,896]{2,0,1:T(2,128)(2,1)}), bf16[1,2304,896]{2,0,1:T(2,128)(2,1)}) %all-gather.37.cloned.1.call-update) | async-done | bytes 4128784 | tf_op jit(solution)/vmap(jvp())/squeeze | solution.py:27
  362.7 16.8 %fusion.28 = bf16[1,2048,2304]{2,1,0:T(8,128)(2,1)} fusion(bf16[1,2304,896]{2,0,1:T(2,128)(2,1)} %all-gather.37.cloned.1.call-done, bf16[1,2048,896]{2,1,0:T(8,128)(2,1)} %param), kind=kOutput, calls=%fused_computation.44 | convolution fusion | flops 8460435456 | bytes 17235968 | tf_op jit(solution)/vmap(transpose(jvp()))/dot_general | solution.py:9
  379.5 17.6 %fusion.24 = f32[2304,896]{0,1:T(8,128)} fusion(bf16[1,2048,2304]{2,1,0:T(8,128)(2,1)} %fusion.28, f32[2048,2304]{1,0:T(8,128)} %fusion.51, bf16[1,2048,896]{1,2,0:T(8,128)(2,1)S(1)} %copy-done.8, f32[2048]{0:T(1024)S(1)} %bitcast.251), kind=kOutput, calls=%fused_computation.32 | convolution fusion | flops 8489533440 | bytes 40247296 | tf_op jit(solution)/vmap(transpose(jvp()))/dot_general | solution.py:21
  397.1 36.1 %all-gather.39.cloned.1.call-done = bf16[1,896,2304]{2,0,1:T(2,128)(2,1)} async-done(((bf16[1,7,2304]{2,0,1:T(2,128)(2,1)}), bf16[1,896,2304]{2,0,1:T(2,128)(2,1)}) %all-gather.39.cloned.1.call-update) | async-done | bytes 4128784 | tf_op jit(solution)/vmap(jvp())/squeeze | solution.py:27
  433.2 14.1 fusion.44
  447.3 19.0 %fusion.8 = bf16[2048,2304]{1,0:T(8,128)(2,1)S(1)} fusion(f32[2048,2304]{1,0:T(8,128)} %fusion.51, f32[2048,2304]{1,0:T(8,128)S(1)} %fusion.44, bf16[1,2048,2304]{2,1,0:T(8,128)(2,1)} %fusion.28), kind=kLoop, calls=%fused_computation.10 | loop fusion | flops 56623104 | bytes 56623104
  469.8 12.9 fusion.88
  482.7 16.4 %fusion.49 = bf16[2048,896]{0,1:T(8,128)(2,1)} fusion(bf16[2048,2304]{1,0:T(8,128)(2,1)} %copy-done.7, bf16[1,896,2304]{2,0,1:T(2,128)(2,1)} %all-gather.35.cloned.1.call-done), kind=kOutput, calls=%fused_computation.66 | convolution fusion | flops 8455716864 | bytes 17235968 | tf_op jit(solution)/vmap(transpose(jvp()))/dot_general | solution.py:20
  499.1 18.3 %fusion.43 = (f32[2048]{0:T(1024)S(1)}, bf16[2048,896]{0,1:T(8,128)(2,1)S(1)}) fusion(bf16[1,2048,896]{1,2,0:T(8,128)(2,1)S(1)} %copy-done.9, bf16[2048,896]{0,1:T(8,128)(2,1)} %fusion.49, bf16[1,896,2304]{2,0,1:T(2,128)(2,1)} %all-gather.39.cloned.1.call-done, bf16[1,2048,2304]{2,1,0:T(8,128)(2,1)} %fusion.28, f32[2048,2304]{1,0:T(8,128)} %fusion.51), kind=kOutput, calls=%fused_computation.60 | convolution fusion | flops 8495036416 | bytes 43458560 | tf_op jit(solution)/vmap(transpose(jvp()))/dot_general | solution.py:21
  522.4 15.8 %fusion.29 = bf16[1,2048,2304]{2,1,0:T(8,128)(2,1)} fusion(bf16[1,2048,896]{1,2,0:T(8,128)(2,1)S(1)} %fusion.66, bf16[1,2304,896]{2,0,1:T(2,128)(2,1)} %all-gather.33.cloned.1.call-done), kind=kOutput, calls=%fused_computation.45 | convolution fusion | flops 8460435456 | bytes 17235968 | tf_op jit(solution)/vmap(transpose(jvp()))/dot_general | solution.py:9
  538.1 17.9 %fusion.20 = f32[2304,896]{0,1:T(8,128)} fusion(bf16[1,2048,2304]{2,1,0:T(8,128)(2,1)} %fusion.29, f32[2048,2304]{1,0:T(8,128)} %fusion.61, bf16[1,2048,896]{1,2,0:T(8,128)(2,1)S(1)} %copy-done.1, f32[2048]{0:T(1024)S(1)} %bitcast.247), kind=kOutput, calls=%fused_computation.30 | convolution fusion | flops 8489533440 | bytes 40247296 | tf_op jit(solution)/vmap(transpose(jvp()))/dot_general | solution.py:21
  556.1 16.3 %fusion.11 = bf16[2048,2304]{1,0:T(8,128)(2,1)S(1)} fusion(f32[2048,2304]{1,0:T(8,128)} %fusion.61, f32[2048,2304]{1,0:T(8,128)} %fusion.57, bf16[1,2048,2304]{2,1,0:T(8,128)(2,1)} %fusion.29), kind=kLoop, calls=%fused_computation.13 | loop fusion | flops 56623104 | bytes 56623104
  575.9 11.4 fusion.83
  587.3 345.8 %fusion.113 = (f32[2304,8]{0,1:T(8,128)S(1)}, f32[2304,8]{0,1:T(8,128)S(1)}, f32[2304,8]{0,1:T(8,128)S(1)}, f32[2304,8]{0,1:T(8,128)S(1)}) fusion(f32[2304,896]{0,1:T(8,128)} %fusion.83, f32[2304,896]{0,1:T(8,128)} %fusion.88, f32[2304,896]{0,1:T(8,128)} %fusion.20, f32[2304,896]{0,1:T(8,128)} %fusion.24), kind=kCustom, calls=%all-reduce-scatter.4 | all-reduce-scatter fusion | flops 9437185 | bytes 33325056
  935.0 26.0 %collective-permute-start.47 = (bf16[2304,7]{0,1:T(8,128)(2,1)S(1)}, bf16[2304,7]{0,1:T(8,128)(2,1)S(1)}, u32[]{:S(2)}, u32[]{:S(2)}) collective-permute-start(bf16[2304,7]{0,1:T(8,128)(2,1)S(1)} %slice.26), channel_id=1, source_target_pairs={{0,16},{1,17},{2,18},{3,19},{4,20},{5,21},{6,22},{7,23},{8,24},{9,... | collective-permute-start | bytes 96776
  970.8 16.9 %fusion.59 = bf16[2048,896]{0,1:T(8,128)(2,1)} fusion(bf16[2048,2304]{1,0:T(8,128)(2,1)} %copy-done.6, bf16[1,896,2304]{2,0,1:T(2,128)(2,1)} %all-gather.29.cloned.1.call-done), kind=kOutput, calls=%fused_computation.76 | convolution fusion | flops 8455716864 | bytes 17235968 | tf_op jit(solution)/vmap(transpose(jvp()))/dot_general | solution.py:20
  987.7 18.5 %fusion.40 = (f32[2048]{0:T(1024)S(1)}, bf16[2048,896]{0,1:T(8,128)(2,1)}) fusion(bf16[1,2048,896]{1,2,0:T(8,128)(2,1)S(1)} %copy-done.2, bf16[2048,896]{0,1:T(8,128)(2,1)} %fusion.59, bf16[1,896,2304]{2,0,1:T(2,128)(2,1)} %all-gather.31.cloned.1.call-done, bf16[1,2048,2304]{2,1,0:T(8,128)(2,1)S(1)} %bitcast.238, f32[2048,2304]{1,0:T(8,128)} %fusion.61), kind=kOutput, calls=%fused_computation.57 | convolution fusion | flops 8495036416 | bytes 43458560 | tf_op jit(solution)/vmap(transpose(jvp()))/dot_general | solution.py:21
  1012.0 15.4 %collective-permute-start.36 = (bf16[2304,8]{0,1:T(8,128)(2,1)S(1)}, bf16[2304,8]{0,1:T(8,128)(2,1)S(1)}, u32[]{:S(2)}, u32[]{:S(2)}) collective-permute-start(bf16[2304,8]{0,1:T(8,128)(2,1)S(1)} %convert.170), channel_id=1, source_target_pairs={{0,5},{1,6},{2,7},{3,8},{4,9},{5,10},{6,11},{7,12},{8,13},{9,14},{... | collective-permute-start | bytes 110600
  1027.4 20.4 %fusion.32 = f32[2304,896]{1,0:T(8,128)} fusion(f32[2048,2304]{1,0:T(8,128)} %copy-done.3, f32[2048,2304]{1,0:T(8,128)} %fusion.51, bf16[1,2048,896]{2,1,0:T(8,128)(2,1)} %param), kind=kOutput, calls=%fused_computation.48 | convolution fusion | flops 8484028416 | bytes 49676288 | tf_op jit(solution)/vmap(transpose(jvp()))/dot_general | solution.py:9
  1055.0 33.9 %collective-permute-start.40 = (bf16[2304,8]{0,1:T(8,128)(2,1)S(1)}, bf16[2304,8]{0,1:T(8,128)(2,1)S(1)}, u32[]{:S(2)}, u32[]{:S(2)}) collective-permute-start(bf16[2304,8]{0,1:T(8,128)(2,1)S(1)} %convert.170), channel_id=1, source_target_pairs={{0,9},{1,10},{2,11},{3,12},{4,13},{5,14},{6,15},{7,16},{8,17},{9,1... | collective-permute-start | bytes 110600
  1097.0 15.7 %fusion.67 = f32[896,2304]{0,1:T(8,128)} fusion(bf16[2048,2304]{1,0:T(8,128)(2,1)} %fusion.30, bf16[1,2048,896]{1,2,0:T(8,128)(2,1)} %copy-done.5), kind=kOutput, calls=%fused_computation.84 | convolution fusion | flops 8455716864 | bytes 21364736 | tf_op jit(solution)/vmap(transpose(jvp()))/dot_general | solution.py:9
  1127.9 126.7 %all-reduce.19 = (bf16[896,2304]{0,1:T(8,128)(2,1)}, bf16[2304,896]{1,0:T(8,128)(2,1)}) all-reduce(f32[896,2304]{0,1:T(8,128)} %fusion.67, f32[2304,896]{1,0:T(8,128)} %fusion.32), channel_id=29, replica_groups=mesh['axis_0'=128] {'axis_0'}, use_global_device_ids=true, to_apply=%add.5.clone.clone | all-reduce | flops 4128768 | bytes 24772608
  1289.3 9.1 fusion.65
  (214 shorter events, 234.5 us)
Async XLA Ops:
  7.2 74.4 %all-gather.29.cloned.1.call-start = ((), (), s32[]{:S(2)}) async-start(), calls=%async_computation | async-start | bytes 8322048 | tf_op jit(solution)/vmap(jvp())/squeeze | solution.py:27
  8.9 143.3 %all-gather.31.cloned.1.call-start = ((), (), s32[]{:S(2)}) async-start(), calls=%async_computation.1 | async-start | bytes 8322048 | tf_op jit(solution)/vmap(jvp())/squeeze | solution.py:27
  10.7 211.6 %all-gather.33.cloned.1.call-start = ((), (), s32[]{:S(2)}) async-start(), calls=%async_computation.2 | async-start | bytes 8322048 | tf_op jit(solution)/vmap(jvp())/squeeze | solution.py:27
  12.4 280.4 %all-gather.35.cloned.1.call-start = ((), (), s32[]{:S(2)}) async-start(), calls=%async_computation.3 | async-start | bytes 8322048 | tf_op jit(solution)/vmap(jvp())/squeeze | solution.py:27
  13.0 349.7 %all-gather.37.cloned.1.call-start = ((), (), s32[]{:S(2)}) async-start(), calls=%async_computation.4 | async-start | bytes 8322048 | tf_op jit(solution)/vmap(jvp())/squeeze | solution.py:27
  13.6 419.6 %all-gather.39.cloned.1.call-start = ((), (), s32[]{:S(2)}) async-start(), calls=%async_computation.5 | async-start | bytes 8322048 | tf_op jit(solution)/vmap(jvp())/squeeze | solution.py:27
  933.1 114.7 %collective-permute-start.32 = (bf16[2304,8]{0,1:T(8,128)(2,1)S(1)}, bf16[2304,8]{0,1:T(8,128)(2,1)S(1)}, u32[]{:S(2)}, u32[]{:S(2)}) collective-permute-start(bf16[2304,8]{0,1:T(8,128)(2,1)S(1)} %convert.170), channel_id=1, source_target_pairs={{0,1},{1,2},{2,3},{3,4},{4,5},{5,6},{6,7},{7,8},{8,9},{9,10},{10,1... | collective-permute-start | bytes 110600
  935.0 71.1 %collective-permute-start.47 = (bf16[2304,7]{0,1:T(8,128)(2,1)S(1)}, bf16[2304,7]{0,1:T(8,128)(2,1)S(1)}, u32[]{:S(2)}, u32[]{:S(2)}) collective-permute-start(bf16[2304,7]{0,1:T(8,128)(2,1)S(1)} %slice.26), channel_id=1, source_target_pairs={{0,16},{1,17},{2,18},{3,19},{4,20},{5,21},{6,22},{7,23},{8,24},{9,... | collective-permute-start | bytes 96776
  961.1 47.0 %collective-permute-start.63 = (bf16[2304,7]{0,1:T(8,128)(2,1)S(1)}, bf16[2304,7]{0,1:T(8,128)(2,1)S(1)}, u32[]{:S(2)}, u32[]{:S(2)}) collective-permute-start(bf16[2304,7]{0,1:T(8,128)(2,1)S(1)} %slice.27), channel_id=1, source_target_pairs={{0,16},{1,17},{2,18},{3,19},{4,20},{5,21},{6,22},{7,23},{8,24},{9,... | collective-permute-start | bytes 96776
  963.0 47.0 %collective-permute-start.15 = (bf16[2304,7]{0,1:T(8,128)(2,1)S(1)}, bf16[2304,7]{0,1:T(8,128)(2,1)S(1)}, u32[]{:S(2)}, u32[]{:S(2)}) collective-permute-start(bf16[2304,7]{0,1:T(8,128)(2,1)S(1)} %slice.24), channel_id=1, source_target_pairs={{0,16},{1,17},{2,18},{3,19},{4,20},{5,21},{6,22},{7,23},{8,24},{9,... | collective-permute-start | bytes 96776
  968.4 43.5 %collective-permute-start.31 = (bf16[2304,7]{0,1:T(8,128)(2,1)S(1)}, bf16[2304,7]{0,1:T(8,128)(2,1)S(1)}, u32[]{:S(2)}, u32[]{:S(2)}) collective-permute-start(bf16[2304,7]{0,1:T(8,128)(2,1)S(1)} %slice.25), channel_id=1, source_target_pairs={{0,16},{1,17},{2,18},{3,19},{4,20},{5,21},{6,22},{7,23},{8,24},{9,... | collective-permute-start | bytes 96776
  1006.2 44.1 %collective-permute-start.33 = (bf16[2304,8]{0,1:T(8,128)(2,1)S(1)}, bf16[2304,8]{0,1:T(8,128)(2,1)S(1)}, u32[]{:S(2)}, u32[]{:S(2)}) collective-permute-start(bf16[2304,8]{0,1:T(8,128)(2,1)S(1)} %convert.170), channel_id=1, source_target_pairs={{0,2},{1,3},{2,4},{3,5},{4,6},{5,7},{6,8},{7,9},{8,10},{9,11},{10,... | collective-permute-start | bytes 110600
  1008.1 44.1 %collective-permute-start.34 = (bf16[2304,8]{0,1:T(8,128)(2,1)S(1)}, bf16[2304,8]{0,1:T(8,128)(2,1)S(1)}, u32[]{:S(2)}, u32[]{:S(2)}) collective-permute-start(bf16[2304,8]{0,1:T(8,128)(2,1)S(1)} %convert.170), channel_id=1, source_target_pairs={{0,3},{1,4},{2,5},{3,6},{4,7},{5,8},{6,9},{7,10},{8,11},{9,12},{10... | collective-permute-start | bytes 110600
  1010.0 45.0 %collective-permute-start.35 = (bf16[2304,8]{0,1:T(8,128)(2,1)S(1)}, bf16[2304,8]{0,1:T(8,128)(2,1)S(1)}, u32[]{:S(2)}, u32[]{:S(2)}) collective-permute-start(bf16[2304,8]{0,1:T(8,128)(2,1)S(1)} %convert.170), channel_id=1, source_target_pairs={{0,4},{1,5},{2,6},{3,7},{4,8},{5,9},{6,10},{7,11},{8,12},{9,13},{1... | collective-permute-start | bytes 110600
  1012.0 77.0 %collective-permute-start.36 = (bf16[2304,8]{0,1:T(8,128)(2,1)S(1)}, bf16[2304,8]{0,1:T(8,128)(2,1)S(1)}, u32[]{:S(2)}, u32[]{:S(2)}) collective-permute-start(bf16[2304,8]{0,1:T(8,128)(2,1)S(1)} %convert.170), channel_id=1, source_target_pairs={{0,5},{1,6},{2,7},{3,8},{4,9},{5,10},{6,11},{7,12},{8,13},{9,14},{... | collective-permute-start | bytes 110600
  1047.8 64.9 %collective-permute-start.37 = (bf16[2304,8]{0,1:T(8,128)(2,1)S(1)}, bf16[2304,8]{0,1:T(8,128)(2,1)S(1)}, u32[]{:S(2)}, u32[]{:S(2)}) collective-permute-start(bf16[2304,8]{0,1:T(8,128)(2,1)S(1)} %convert.170), channel_id=1, source_target_pairs={{0,6},{1,7},{2,8},{3,9},{4,10},{5,11},{6,12},{7,13},{8,14},{9,15},... | collective-permute-start | bytes 110600
  1050.3 65.7 %collective-permute-start.38 = (bf16[2304,8]{0,1:T(8,128)(2,1)S(1)}, bf16[2304,8]{0,1:T(8,128)(2,1)S(1)}, u32[]{:S(2)}, u32[]{:S(2)}) collective-permute-start(bf16[2304,8]{0,1:T(8,128)(2,1)S(1)} %convert.170), channel_id=1, source_target_pairs={{0,7},{1,8},{2,9},{3,10},{4,11},{5,12},{6,13},{7,14},{8,15},{9,16}... | collective-permute-start | bytes 110600
  1052.2 68.1 %collective-permute-start.39 = (bf16[2304,8]{0,1:T(8,128)(2,1)S(1)}, bf16[2304,8]{0,1:T(8,128)(2,1)S(1)}, u32[]{:S(2)}, u32[]{:S(2)}) collective-permute-start(bf16[2304,8]{0,1:T(8,128)(2,1)S(1)} %convert.170), channel_id=1, source_target_pairs={{0,8},{1,9},{2,10},{3,11},{4,12},{5,13},{6,14},{7,15},{8,16},{9,17... | collective-permute-start | bytes 110600
  1055.0 68.1 %collective-permute-start.40 = (bf16[2304,8]{0,1:T(8,128)(2,1)S(1)}, bf16[2304,8]{0,1:T(8,128)(2,1)S(1)}, u32[]{:S(2)}, u32[]{:S(2)}) collective-permute-start(bf16[2304,8]{0,1:T(8,128)(2,1)S(1)} %convert.170), channel_id=1, source_target_pairs={{0,9},{1,10},{2,11},{3,12},{4,13},{5,14},{6,15},{7,16},{8,17},{9,1... | collective-permute-start | bytes 110600
  1089.0 36.1 %collective-permute-start.41 = (bf16[2304,8]{0,1:T(8,128)(2,1)S(1)}, bf16[2304,8]{0,1:T(8,128)(2,1)S(1)}, u32[]{:S(2)}, u32[]{:S(2)}) collective-permute-start(bf16[2304,8]{0,1:T(8,128)(2,1)S(1)} %convert.170), channel_id=1, source_target_pairs={{0,10},{1,11},{2,12},{3,13},{4,14},{5,15},{6,16},{7,17},{8,18},{9,... | collective-permute-start | bytes 110600
  1112.7 141.9 %collective-permute-start.42 = (bf16[2304,8]{0,1:T(8,128)(2,1)S(1)}, bf16[2304,8]{0,1:T(8,128)(2,1)S(1)}, u32[]{:S(2)}, u32[]{:S(2)}) collective-permute-start(bf16[2304,8]{0,1:T(8,128)(2,1)S(1)} %convert.170), channel_id=1, source_target_pairs={{0,11},{1,12},{2,13},{3,14},{4,15},{5,16},{6,17},{7,18},{8,19},{9,... | collective-permute-start | bytes 110600
  1116.0 141.2 %collective-permute-start.43 = (bf16[2304,8]{0,1:T(8,128)(2,1)S(1)}, bf16[2304,8]{0,1:T(8,128)(2,1)S(1)}, u32[]{:S(2)}, u32[]{:S(2)}) collective-permute-start(bf16[2304,8]{0,1:T(8,128)(2,1)S(1)} %convert.170), channel_id=1, source_target_pairs={{0,12},{1,13},{2,14},{3,15},{4,16},{5,17},{6,18},{7,19},{8,20},{9,... | collective-permute-start | bytes 110600
  1120.3 139.4 %collective-permute-start.44 = (bf16[2304,8]{0,1:T(8,128)(2,1)S(1)}, bf16[2304,8]{0,1:T(8,128)(2,1)S(1)}, u32[]{:S(2)}, u32[]{:S(2)}) collective-permute-start(bf16[2304,8]{0,1:T(8,128)(2,1)S(1)} %convert.170), channel_id=1, source_target_pairs={{0,13},{1,14},{2,15},{3,16},{4,17},{5,18},{6,19},{7,20},{8,21},{9,... | collective-permute-start | bytes 110600
  1123.2 140.5 %collective-permute-start.45 = (bf16[2304,8]{0,1:T(8,128)(2,1)S(1)}, bf16[2304,8]{0,1:T(8,128)(2,1)S(1)}, u32[]{:S(2)}, u32[]{:S(2)}) collective-permute-start(bf16[2304,8]{0,1:T(8,128)(2,1)S(1)} %convert.170), channel_id=1, source_target_pairs={{0,14},{1,15},{2,16},{3,17},{4,18},{5,19},{6,20},{7,21},{8,22},{9,... | collective-permute-start | bytes 110600
  1125.1 142.4 %collective-permute-start.46 = (bf16[2304,8]{0,1:T(8,128)(2,1)S(1)}, bf16[2304,8]{0,1:T(8,128)(2,1)S(1)}, u32[]{:S(2)}, u32[]{:S(2)}) collective-permute-start(bf16[2304,8]{0,1:T(8,128)(2,1)S(1)} %convert.170), channel_id=1, source_target_pairs={{0,15},{1,16},{2,17},{3,18},{4,19},{5,20},{6,21},{7,22},{8,23},{9,... | collective-permute-start | bytes 110600
  1273.2 25.2 %collective-permute-start.53 = (bf16[2304,8]{0,1:T(8,128)(2,1)S(1)}, bf16[2304,8]{0,1:T(8,128)(2,1)S(1)}, u32[]{:S(2)}, u32[]{:S(2)}) collective-permute-start(bf16[2304,8]{0,1:T(8,128)(2,1)S(1)} %convert.171), channel_id=1, source_target_pairs={{0,6},{1,7},{2,8},{3,9},{4,10},{5,11},{6,12},{7,13},{8,14},{9,15},... | collective-permute-start | bytes 110600
  1275.1 25.6 %collective-permute-start.54 = (bf16[2304,8]{0,1:T(8,128)(2,1)S(1)}, bf16[2304,8]{0,1:T(8,128)(2,1)S(1)}, u32[]{:S(2)}, u32[]{:S(2)}) collective-permute-start(bf16[2304,8]{0,1:T(8,128)(2,1)S(1)} %convert.171), channel_id=1, source_target_pairs={{0,7},{1,8},{2,9},{3,10},{4,11},{5,12},{6,13},{7,14},{8,15},{9,16}... | collective-permute-start | bytes 110600
  1277.9 27.5 %collective-permute-start.55 = (bf16[2304,8]{0,1:T(8,128)(2,1)S(1)}, bf16[2304,8]{0,1:T(8,128)(2,1)S(1)}, u32[]{:S(2)}, u32[]{:S(2)}) collective-permute-start(bf16[2304,8]{0,1:T(8,128)(2,1)S(1)} %convert.171), channel_id=1, source_target_pairs={{0,8},{1,9},{2,10},{3,11},{4,12},{5,13},{6,14},{7,15},{8,16},{9,17... | collective-permute-start | bytes 110600
  1280.5 31.1 %collective-permute-start.56 = (bf16[2304,8]{0,1:T(8,128)(2,1)S(1)}, bf16[2304,8]{0,1:T(8,128)(2,1)S(1)}, u32[]{:S(2)}, u32[]{:S(2)}) collective-permute-start(bf16[2304,8]{0,1:T(8,128)(2,1)S(1)} %convert.171), channel_id=1, source_target_pairs={{0,9},{1,10},{2,11},{3,12},{4,13},{5,14},{6,15},{7,16},{8,17},{9,1... | collective-permute-start | bytes 110600
  1284.4 29.7 %collective-permute-start.57 = (bf16[2304,8]{0,1:T(8,128)(2,1)S(1)}, bf16[2304,8]{0,1:T(8,128)(2,1)S(1)}, u32[]{:S(2)}, u32[]{:S(2)}) collective-permute-start(bf16[2304,8]{0,1:T(8,128)(2,1)S(1)} %convert.171), channel_id=1, source_target_pairs={{0,10},{1,11},{2,12},{3,13},{4,14},{5,15},{6,16},{7,17},{8,18},{9,... | collective-permute-start | bytes 110600
  1338.5 22.4 %collective-permute-start.2 = (bf16[2304,8]{0,1:T(8,128)(2,1)S(1)}, bf16[2304,8]{0,1:T(8,128)(2,1)S(1)}, u32[]{:S(2)}, u32[]{:S(2)}) collective-permute-start(bf16[2304,8]{0,1:T(8,128)(2,1)S(1)} %convert.172), channel_id=1, source_target_pairs={{0,3},{1,4},{2,5},{3,6},{4,7},{5,8},{6,9},{7,10},{8,11},{9,12},{10... | collective-permute-start | bytes 110600
  1340.4 22.4 %collective-permute-start.3 = (bf16[2304,8]{0,1:T(8,128)(2,1)S(1)}, bf16[2304,8]{0,1:T(8,128)(2,1)S(1)}, u32[]{:S(2)}, u32[]{:S(2)}) collective-permute-start(bf16[2304,8]{0,1:T(8,128)(2,1)S(1)} %convert.172), channel_id=1, source_target_pairs={{0,4},{1,5},{2,6},{3,7},{4,8},{5,9},{6,10},{7,11},{8,12},{9,13},{1... | collective-permute-start | bytes 110600
  (57 other events, 1077.0 us)
Sparse Core Ops, SparseCore 0:
  10.9 70.6 all-gather.28
  85.1 67.0 all-gather.30
  155.2 67.0 all-gather.32
  225.7 67.0 all-gather.34
  295.6 67.0 all-gather.36
  366.1 67.0 all-gather.38
where the time goes:
time: 1430 us; the launch traced here: 1420 us
  blocking collectives  472 us (33%)
  waiting for transfers between devices  291 us (20%)
  matrix products  282 us (20%)
  starting transfers between devices  250 us (17%)
  other arithmetic  64.4 us (5%)
  local copies, waits for them, and re-layouts  47.1 us (3%)
  between operations  15.9 us (1%)
    unnamed x2, blocking collectives  472 us
    squeeze x6, waiting for transfers between devices, stack(): h = layer(h, {name: w[number] for name, w in weights.items()})  284 us
    unnamed x64, starting transfers between devices  250 us
    dot_general x6, matrix products, layer(): up = jnp.dot(a, w['w_up'], preferred_element_type=jnp.float32)  104 us
    dot_general x6, matrix products, layer(): gate = jnp.dot(a, w['w_gate'], preferred_element_type=jnp.float32)  93.2 us
    dot_general x5, matrix products, matmul(): jnp.dot(a, w, preferred_element_type=jnp.float32).astype(jnp.bfloat16)  84.7 us
    unnamed x8, other arithmetic  49.4 us
    unnamed x52, local copies, waits for them, and re-layouts  40.3 us
  transfers between devices with their start and end apart: 70, of which 8 were waited for; matrix products, arithmetic and copies ran while one was open for 16% of the time, Pallas kernels for 0%

commit v1 on v0

v1 whole, which is shorter than its diff:
```python
import functools

import jax
import jax.numpy as jnp
import numpy as np
from jax import lax
from jax.experimental import pallas as pl
from jax.experimental.pallas import tpu as pltpu
from jax.sharding import PartitionSpec as P

D = 896
FF = 2304
TOK = 2048
C = FF + 1024
BF = jnp.bfloat16
F32 = jnp.float32
MESH = pl.DeviceIdType.MESH
ORDERS = ((0, 1, 2), (1, 2, 0), (2, 0, 1))
ANY = pl.BlockSpec(memory_space=pl.ANY)
VMEM = pl.BlockSpec(memory_space=pltpu.VMEM)


def colours(start, width):
    tiles = width // 128
    out, at = [], start
    for k in range(3):
        n = tiles // 3 + (1 if k < tiles % 3 else 0)
        first = (n + 1) // 2
        out.append(((at, first * 128), (at + first * 128, (n - first) * 128)))
        at += n * 128
    return out


def where():
    me = lax.axis_index("dp")
    return (me // 32, lax.rem(me // 8, 4), lax.rem(me // 2, 4)), lax.rem(me, 2)


def number(xyz, c):
    return ((xyz[0] * 4 + xyz[1]) * 4 + xyz[2]) * 2 + c


def moved(xyz, axis, by):
    out = list(xyz)
    out[axis] = lax.rem(xyz[axis] + by + 4, 4)
    return tuple(out)


def rendezvous(xyz, c):
    barrier = pltpu.get_barrier_semaphore()
    for axis in range(3):
        for by in (1, -1):
            pl.semaphore_signal(barrier, inc=1, device_id={"dp": number(moved(xyz, axis, by), c)}, device_id_type=MESH)
    pl.semaphore_signal(barrier, inc=1, device_id={"dp": number(xyz, 1 - c)}, device_id_type=MESH)
    pl.semaphore_wait(barrier, 7)


def remote(src, dst, send, recv, xyz, c):
    return pltpu.make_async_remote_copy(
        src_ref=src, dst_ref=dst, send_sem=send, recv_sem=recv, device_id={"dp": number(xyz, c)}, device_id_type=MESH
    )


class Gather:
    def __init__(self, cols, shard, g, send, recv, dsend, drecv, lsem):
        self.cols, self.shard, self.g = cols, shard, g
        self.send, self.recv, self.dsend, self.drecv, self.lsem = send, recv, dsend, drecv, lsem
        self.xyz, self.c = where()
        self.pending, self.partner = [], []

    def block(self, k, phase, xyz, half):
        order = ORDERS[k]
        at = [slice(None) if axis in order[:phase] else xyz[axis] for axis in range(3)]
        start, size = self.cols[k][half]
        return self.g.at[at[0], at[1], at[2], self.c, :, pl.ds(start, size)]

    def copy(self, k, phase, owner, half, to, slot, first=False):
        here = self.block(k, phase, owner, half)
        start, size = self.cols[k][half]
        src = self.shard.at[:, pl.ds(start, size)] if first else here
        return remote(src, here, self.send.at[k, phase, slot], self.recv.at[k, phase, slot], to, self.c)

    def local(self):
        return pltpu.make_async_copy(self.shard, self.g.at[self.xyz[0], self.xyz[1], self.xyz[2], self.c], self.lsem)

    def give(self, k, phase, owner, half, slot):
        here = self.block(k, phase, owner, half)
        copy = remote(here, here, self.dsend.at[k, slot], self.drecv.at[k, slot], self.xyz, 1 - self.c)
        copy.start()
        there = self.block_of_partner(k, phase, owner, half)
        self.partner.append((copy, remote(there, there, self.dsend.at[k, slot], self.drecv.at[k, slot], self.xyz, 1 - self.c)))

    def block_of_partner(self, k, phase, owner, half):
        order = ORDERS[k]
        at = [slice(None) if axis in order[:phase] else owner[axis] for axis in range(3)]
        start, size = self.cols[k][half]
        return self.g.at[at[0], at[1], at[2], 1 - self.c, :, pl.ds(start, size)]

    def begin(self, phase):
        if phase == 0:
            self.local().start()
        if phase == 1:
            self.local().wait()
        for k in range(3):
            axis = ORDERS[k][phase]
            right, left = moved(self.xyz, axis, 1), moved(self.xyz, axis, -1)
            for to, half, slot in ((right, 0, 0), (left, 1, 3), (right, 1, 1), (left, 0, 2)):
                copy = self.copy(k, phase, self.xyz, half, to, slot, phase == 0)
                copy.start()
                self.pending.append(copy)
            if phase == 2:
                for half in range(2):
                    self.give(k, 2, self.xyz, half, half)

    def relay(self, phase):
        for k in range(3):
            axis = ORDERS[k][phase]
            right, left = moved(self.xyz, axis, 1), moved(self.xyz, axis, -1)
            for owner, to, half, slot, out in ((left, right, 0, 0, 4), (right, left, 1, 3, 5)):
                self.copy(k, phase, owner, half, to, slot).wait_recv()
                copy = self.copy(k, phase, owner, half, to, out)
                copy.start()
                self.pending.append(copy)
                if phase == 2:
                    self.give(k, 2, owner, half, 2 + half)

    def finish(self, phase):
        for k in range(3):
            axis = ORDERS[k][phase]
            right, left, far = moved(self.xyz, axis, 1), moved(self.xyz, axis, -1), moved(self.xyz, axis, 2)
            for owner, half, slot, give in ((left, 1, 1, 4), (right, 0, 2, 5), (far, 0, 4, 6), (far, 1, 5, 7)):
                self.copy(k, phase, owner, half, owner, slot).wait_recv()
                if phase == 2:
                    self.give(k, 2, owner, half, give)

    def end(self):
        for mine, theirs in self.partner:
            theirs.wait_recv()
            mine.wait_send()
        for copy in self.pending:
            copy.wait_send()

    def steps(self):
        out = []
        for phase in range(3):
            out += [functools.partial(f, phase) for f in (self.begin, self.relay, self.finish)]
        return out + [self.end]


GATHER_SEMS = [
    pltpu.SemaphoreType.DMA((3, 3, 6)),
    pltpu.SemaphoreType.DMA((3, 3, 6)),
    pltpu.SemaphoreType.DMA((3, 8)),
    pltpu.SemaphoreType.DMA((3, 8)),
    pltpu.SemaphoreType.DMA,
]


def gather_kernel(cols, shard, g, *sems):
    gather = Gather(cols, shard, g, *sems)
    rendezvous(gather.xyz, gather.c)
    for step in gather.steps():
        step()


def gather_call(shard, collective_id):
    width = shard.shape[1]
    return pl.pallas_call(
        functools.partial(gather_kernel, colours(0, width)),
        out_shape=jax.ShapeDtypeStruct((4, 4, 4, 2, 16, width), BF),
        in_specs=[VMEM],
        out_specs=ANY,
        scratch_shapes=GATHER_SEMS,
        compiler_params=pltpu.CompilerParams(collective_id=collective_id, has_side_effects=True),
        name="gather",
    )(shard)


class Scatter:
    def __init__(self, cols, d, out, own, pair, keep, one, left2, right2, next_, send, recv, dsend, drecv, lsem):
        self.cols, self.d, self.out, self.own, self.pair = cols, d, out, own, pair
        self.keep, self.one, self.l2, self.r2, self.next = keep, one, left2, right2, next_
        self.send, self.recv, self.dsend, self.drecv, self.lsem = send, recv, dsend, drecv, lsem
        self.xyz, self.c = where()
        self.pending = []

    def local(self, k):
        (start, n0), (_, n1) = self.cols[k]
        at = pl.ds(start, n0 + n1)
        return pltpu.make_async_copy(self.d.at[:, :, :, self.c, :, at], self.own.at[:, :, :, :, at], self.lsem.at[k])

    def swap(self, k):
        (start, n0), (_, n1) = self.cols[k]
        at = pl.ds(start, n0 + n1)
        return remote(
            self.d.at[:, :, :, 1 - self.c, :, at], self.pair.at[:, :, :, :, at], self.dsend.at[k], self.drecv.at[k], self.xyz, 1 - self.c
        )

    def begin_swap(self):
        for k in range(3):
            self.local(k).start()
            self.swap(k).start()

    def cut(self, k, half):
        start, size = self.cols[k][half]
        return pl.ds(start, size)

    def both(self, k):
        (start, n0), (_, n1) = self.cols[k]
        return pl.ds(start, n0 + n1)

    def add_swap(self, k):
        self.local(k).wait()
        self.swap(k).wait_recv()
        at, axis = self.both(k), ORDERS[k][0]

        def body(i, _):
            xyz = (i // 16, lax.rem(i // 4, 4), lax.rem(i, 4))
            here = (*xyz, slice(None), at)
            total = self.own[here].astype(F32) + self.pair[here].astype(F32)
            self.own[here] = total.astype(BF)
            rest = [xyz[a] for a in range(3) if a != axis]

            @pl.when(xyz[axis] == self.xyz[axis])
            def _():
                self.keep[0][(*rest, slice(None), at)] = total

            return 0

        lax.fori_loop(0, 64, body, 0)

    def source(self, k, phase, where_):
        order = ORDERS[k]
        if phase == 0:
            return [where_ if a == order[0] else slice(None) for a in range(3)]
        if phase == 1:
            rest = [a for a in range(3) if a != order[0]]
            return [where_ if a == order[1] else slice(None) for a in rest]
        return [where_]

    def buf(self, phase):
        return self.own if phase == 0 else self.next[phase - 1]

    def copy(self, k, phase, half, slot, to, to_at, dst):
        src = self.buf(phase).at[(*self.source(k, phase, to_at), slice(None), self.cut(k, half))]
        lead = [slice(None)] * (2 - phase)
        there = dst[phase].at[(*lead, slice(None), self.cut(k, half))]
        return remote(src, there, self.send.at[k, phase, slot], self.recv.at[k, phase, slot], to, self.c)

    def sides(self, k, phase):
        axis = ORDERS[k][phase]
        right, left = moved(self.xyz, axis, 1), moved(self.xyz, axis, -1)
        return right, left, right[axis], left[axis], lax.rem(self.xyz[axis] + 2, 4)

    def first(self, k, phase):
        right, left, ri, li, far = self.sides(k, phase)
        for copy in (
            self.copy(k, phase, 0, 0, right, far, self.one),
            self.copy(k, phase, 1, 1, left, far, self.one),
            self.copy(k, phase, 1, 2, right, ri, self.l2),
            self.copy(k, phase, 0, 3, left, li, self.r2),
        ):
            copy.start()
            self.pending.append(copy)

    def shards(self, phase):
        return (16, 4, 1)[phase]

    def lead(self, phase, i):
        return ((i // 4, lax.rem(i, 4)), (i,), ())[phase]

    def second(self, k, phase):
        right, left, ri, li, far = self.sides(k, phase)
        for half, slot, to, to_at, dst, out in ((0, 0, right, ri, self.l2, 4), (1, 1, left, li, self.r2, 5)):
            self.copy(k, phase, half, slot, to, far, self.one).wait_recv()
            at, buf = self.cut(k, half), self.buf(phase)
            where_ = self.source(k, phase, to_at)

            def body(i, _):
                lead = self.lead(phase, i)
                it = iter(lead)
                idx = tuple(next(it) if isinstance(w, slice) else w for w in where_)
                here = (*idx, slice(None), at)
                got = self.one[phase][(*lead, slice(None), at)]
                buf[here] = (buf[here].astype(F32) + got.astype(F32)).astype(BF)
                return 0

            lax.fori_loop(0, self.shards(phase), body, 0)
            copy = self.copy(k, phase, half, out, to, to_at, dst)
            copy.start()
            self.pending.append(copy)

    def third(self, k, phase):
        right, left, ri, li, far = self.sides(k, phase)
        for half, slot, dst in ((1, 2, self.l2), (0, 3, self.r2), (0, 4, self.l2), (1, 5, self.r2)):
            self.copy(k, phase, half, slot, right, ri, dst).wait_recv()
        at, order = self.both(k), ORDERS[k]

        def body(i, _):
            lead = self.lead(phase, i)
            here = (*lead, slice(None), at)
            total = self.keep[phase][here] + self.l2[phase][here].astype(F32) + self.r2[phase][here].astype(F32)
            if phase == 2:
                self.out[:, at] = total.astype(BF)
                return 0
            self.next[phase][here] = total.astype(BF)
            if phase == 0:
                rest = [a for a in range(3) if a != order[0]]
                mine = [n for n, a in zip(lead, rest) if a == order[1]][0]
                other = tuple(n for n, a in zip(lead, rest) if a != order[1])
            else:
                mine, other = lead[0], ()

            @pl.when(mine == self.xyz[order[phase + 1]])
            def _():
                self.keep[phase + 1][(*other, slice(None), at)] = total

            return 0

        lax.fori_loop(0, self.shards(phase), body, 0)

    def end(self):
        for k in range(3):
            self.swap(k).wait_send()
        for copy in self.pending:
            copy.wait_send()

    def steps(self):
        out = [self.begin_swap]
        for k in range(3):
            out += [functools.partial(self.add_swap, k), functools.partial(self.first, k, 0)]
        for phase in range(3):
            out += [functools.partial(self.second, k, phase) for k in range(3)]
            for k in range(3):
                out.append(functools.partial(self.third, k, phase))
                if phase < 2:
                    out.append(functools.partial(self.first, k, phase + 1))
        return out + [self.end]


def scatter_scratch(width):
    w = (16, width)
    leads = ((4, 4), (4,), ())
    return [
        pltpu.VMEM((4, 4, 4, *w), BF),
        pltpu.VMEM((4, 4, 4, *w), BF),
        *[pltpu.VMEM((*lead, *w), F32) for lead in leads],
        *[pltpu.VMEM((*lead, *w), BF) for _ in range(3) for lead in leads],
        *[pltpu.VMEM((*lead, *w), BF) for lead in leads[:2]],
        pltpu.SemaphoreType.DMA((3, 3, 6)),
        pltpu.SemaphoreType.DMA((3, 3, 6)),
        pltpu.SemaphoreType.DMA((3,)),
        pltpu.SemaphoreType.DMA((3,)),
        pltpu.SemaphoreType.DMA((3,)),
    ]


def make_scatter(cols, d, out, scratch):
    own, pair = scratch[:2]
    keep, one, l2, r2, next_ = scratch[2:5], scratch[5:8], scratch[8:11], scratch[11:14], scratch[14:16]
    return Scatter(cols, d, out, own, pair, keep, one, l2, r2, next_, *scratch[16:])


def scatter_kernel(cols, d, out, *scratch):
    scatter = make_scatter(cols, d, out, scratch)
    rendezvous(scatter.xyz, scatter.c)
    for step in scatter.steps():
        step()


def scatter_call(d, collective_id):
    width = d.shape[-1]
    return pl.pallas_call(
        functools.partial(scatter_kernel, colours(0, width)),
        out_shape=jax.ShapeDtypeStruct((16, width), BF),
        in_specs=[ANY],
        out_specs=VMEM,
        scratch_shapes=scatter_scratch(width),
        compiler_params=pltpu.CompilerParams(collective_id=collective_id, has_side_effects=True, vmem_limit_bytes=60 * 2**20),
        name="scatter",
    )(d)


def picks():
    gu = np.zeros((224, 256), np.float32)
    main = np.zeros((288, 256), np.float32)
    extra = np.zeros((7, 288, 256), np.float32)
    for d in range(16):
        for j in range(7):
            gu[7 * d + j, 16 * d + j] = 1
            gu[112 + 7 * d + j, 16 * d + 8 + j] = 1
        for r in range(16):
            main[18 * d + r, 16 * d + r] = 1
        for e in range(2):
            for t in range(7):
                extra[t, 18 * d + 16 + e, 16 * d + 7 * e + t] = 1
    return tuple(jnp.asarray(t, BF) for t in (gu, main, extra))


def one_hot(spec, *args):
    return jnp.einsum(spec, *args, preferred_element_type=F32)


def pack_shard(gate, up, down):
    row = ((0, 1), (0, 0))
    gu = jnp.concatenate([jnp.pad(gate, row), jnp.pad(up, row)], 0)
    rest = jnp.pad(down[16:].reshape(14, 128), ((0, 2), (0, 0)))
    return jnp.concatenate([gu, down[:16], rest], 1)


def unpack_shard(p):
    gate, up = p[:7, :FF], p[8:15, :FF]
    down = jnp.concatenate([p[:, FF : FF + D], p[:14, FF + D :].reshape(2, D)], 0)
    return gate, up, down


def unpack_gu(g):
    gu = picks()[0]
    w = one_hot("rk,gkn->grn", gu, g.reshape(8, 256, FF)).astype(BF)
    return w[:, :112].reshape(D, FF), w[:, 112:].reshape(D, FF)


def unpack_down(g):
    _, main, extra = picks()
    g = g.reshape(8, 256, 1024)
    w = one_hot("rk,gkn->grn", main, g[..., :D]).reshape(8, 288, 7, 128) + one_hot("trk,gkn->grtn", extra, g[..., D:])
    return w.astype(BF).reshape(FF, D)


def pack_gu(gate, up):
    gu = picks()[0]
    w = jnp.concatenate([gate.reshape(8, 112, FF), up.reshape(8, 112, FF)], 1)
    return one_hot("rk,grn->gkn", gu, w).astype(BF).reshape(4, 4, 4, 2, 16, FF)


def pack_down(down):
    _, main, extra = picks()
    w = down.reshape(8, 288, D)
    a = one_hot("rk,grn->gkn", main, w)
    b = one_hot("trk,grtn->gkn", extra, w.reshape(8, 288, 7, 128))
    return jnp.concatenate([a, b], -1).astype(BF).reshape(4, 4, 4, 2, 16, 1024)


def matmul(a, w):
    return jnp.dot(a, w, preferred_element_type=F32).astype(BF)


def normed(h):
    wide = h.astype(F32)
    scale = lax.rsqrt(jnp.mean(wide**2, -1, keepdims=True) + 1e-6)
    return (wide * scale).astype(BF)


def layer(h, w):
    a = normed(h)
    gate = jnp.dot(a, w[0], preferred_element_type=F32)
    up = jnp.dot(a, w[1], preferred_element_type=F32)
    return h + matmul((jax.nn.silu(gate) * up).astype(BF), w[2])


def stack(weights, h):
    for w in weights:
        h = layer(h, w)
    return h


def solution(mesh):
    def step(x, dy, gate, up, down):
        shard = jnp.concatenate([pack_shard(gate[n], up[n], down[n]) for n in range(2)], 1)
        g = gather_call(shard, 0)
        weights = []
        for n in range(2):
            part = g[..., n * C : (n + 1) * C]
            weights.append((*unpack_gu(part[..., :FF]), unpack_down(part[..., FF:])))
        _, back = jax.vjp(stack, weights, x[0])
        by_weights, by_x = back(dy[0])
        outs = []
        for n in (1, 0):
            dg, du, dd = by_weights[n]
            d = jnp.concatenate([pack_gu(dg, du), pack_down(dd)], -1)
            outs.append(unpack_shard(scatter_call(d, 1)))
        outs = outs[::-1]
        return (by_x[None], *(jnp.stack([o[i] for o in outs]) for i in range(3)))

    rows = P(None, "dp", None)
    return jax.shard_map(
        step, mesh=mesh, in_specs=(P("dp"), P("dp"), rows, rows, rows), out_specs=(P("dp"), rows, rows, rows), check_vma=False
    )
```

time: 1430 us -> 629 us (0.44)
  blocking collectives: 472 us -> 0 us
  waiting for transfers between devices: 291 us -> 0 us
  starting transfers between devices: 250 us -> 0 us
  Pallas kernels: 0 us -> 172 us
  matrix products: 282 us -> 328 us
  local copies, waits for them, and re-layouts: 47.1 us -> 81.4 us
  other arithmetic: 64.4 us -> 34.5 us
  between operations: 15.9 us -> 1.29 us
    unnamed x2 -> x0, blocking collectives: 472 us -> none
    squeeze x6 -> x0, waiting for transfers between devices: 284 us -> none  [stack(): h = layer(h, {name: w[number] for name, w in weights.items()})]
    unnamed x64 -> x0, starting transfers between devices: 250 us -> none
    pallas_call x0 -> x3, Pallas kernels: none -> 172 us  [the longest x2 99.3 us: scatter_call(): pl.pallas_call(functools.partial(scatter_kernel, colours(0, width)), out_...]
    unnamed x8 -> x2, other arithmetic: 49.4 us -> 0.03 us
    dot_general x17 -> x29, matrix products: 282 us -> 328 us  [the longest x6 104 us: layer(): up = jnp.dot(a, w[1], preferred_element_type=F32)]
    slice x3 -> x12, local copies, waits for them, and re-layouts: 5.04 us -> 29.4 us  [the longest x2 13.6 us: step(): weights.append((*unpack_gu(part[..., :FF]), unpack_down(part[..., FF:])))]
    concatenate x0 -> x2, other arithmetic: none -> 23.9 us  [step(): d = jnp.concatenate([pack_gu(dg, du), pack_down(dd)], -1)]
  transfers between devices with their start and end apart: 70 -> 0, of which waited for: 8 -> 0; matrix products, arithmetic and copies ran while one was open for 16% -> 0% of each run, Pallas kernels for 0% -> 0%
where the time goes in v1:
time: 629 us; the launch traced here: 617 us
  matrix products  328 us (52%)
  Pallas kernels  172 us (27%)
  local copies, waits for them, and re-layouts  81.4 us (13%)
  other arithmetic  34.5 us (5%)
    dot_general x6, matrix products, layer(): up = jnp.dot(a, w[1], preferred_element_type=F32)  104 us
    pallas_call x2, Pallas kernels, scatter_call(): pl.pallas_call(functools.partial(scatter_kernel, colours(0, width)), out_...  99.3 us
    dot_general x5, matrix products, matmul(): return jnp.dot(a, w, preferred_element_type=F32).astype(BF)  91.2 us
    dot_general x6, matrix products, layer(): gate = jnp.dot(a, w[0], preferred_element_type=F32)  91.2 us
    pallas_call x1, Pallas kernels, gather_call(): pl.pallas_call(functools.partial(gather_kernel, colours(0, width)), out_s...  72.5 us
    dot_general x12, matrix products, one_hot(): return jnp.einsum(spec, *args, preferred_element_type=F32)  41.7 us
    unnamed x75, local copies, waits for them, and re-layouts  25.9 us
    concatenate x2, other arithmetic, step(): d = jnp.concatenate([pack_gu(dg, du), pack_down(dd)], -1)  23.9 us

profile of v1, /device:TPU:17, one launch (start us, length us, event | category | flops | bytes accessed | tf_op | source)
XLA Modules:
  0.0 617.2 jit_solution(8101562326588880707)
XLA Ops:
  4.7 6.1 copy.41
  14.3 6.1 copy.40
  20.4 72.5 %gather.1 = bf16[4,4,4,2,16,6656]{5,4,3,2,1,0:T(8,128)(2,1)} custom-call(bf16[16,6656]{1,0:T(8,128)(2,1)} %copy-done.24), custom_call_target="tpu_custom_call" | custom-call | tf_op jit(solution)/shard_map/gather/pallas_call | solution.py:168
  92.9 6.4 %fusion.118 = (bf16[4,4,4,2,16,1024]{5,4,3,2,1,0:T(8,128)(2,1)}, bf16[4,4,4,2,16,1024]{5,4,3,2,1,0:T(8,128)(2,1)}) fusion(bf16[4,4,4,2,16,6656]{5,4,3,2,1,0:T(8,128)(2,1)} %gather.1), kind=kLoop, calls=%fused_computation.147 | loop fusion | bytes 16777216 | tf_op jit(solution)/shard_map/slice | solution.py:474
  99.3 7.3 %fusion.119 = (bf16[4,4,4,2,16,2304]{5,4,3,2,1,0:T(8,128)(2,1)S(1)}, bf16[4,4,4,2,16,2304]{5,4,3,2,1,0:T(8,128)(2,1)S(1)}) fusion(bf16[4,4,4,2,16,6656]{5,4,3,2,1,0:T(8,128)(2,1)} %gather.1), kind=kLoop, calls=%fused_computation.148 | loop fusion | bytes 37748736 | tf_op jit(solution)/shard_map/slice | solution.py:474
  106.6 5.6 convert_bitcast_fusion
  136.7 12.3 %convolution_convert_fusion.1 = bf16[2304,2048]{0,1:T(8,128)(2,1)} fusion(bf16[288,8,7,128]{3,2,1,0:T(8,128)(2,1)S(1)} %bitcast.206, bf16[1,2048,896]{2,1,0:T(8,128)(2,1)S(1)} %copy-done.17), kind=kOutput, calls=%fused_computation.31 | convolution fusion | flops 8460435456 | bytes 17235968 | tf_op jit(solution)/shard_map/transpose(jvp())/dot_general | solution.py:445
  149.1 13.4 %fusion.79 = f32[2048,2304]{1,0:T(8,128)} fusion(bf16[896,2304]{1,0:T(8,128)(2,1)S(1)} %bitcast.207, bf16[1,2048,896]{2,1,0:T(8,128)(2,1)S(1)} %copy-done.16, f32[2048]{0:T(1024)S(1)} %fusion.109), kind=kOutput, calls=%fused_computation.99 | convolution fusion | flops 8461221888 | bytes 26681344 | tf_op jit(solution)/shard_map/jvp()/dot_general | solution.py:456
  162.5 21.3 %multiply_convert_fusion.1 = (bf16[2048,2304]{1,0:T(8,128)(2,1)}, f32[2048,2304]{1,0:T(8,128)}) fusion(f32[2048,2304]{1,0:T(8,128)} %fusion.79, bf16[896,2304]{1,0:T(8,128)(2,1)} %bitcast.209, bf16[1,2048,896]{2,1,0:T(8,128)(2,1)} %param.17, f32[2048]{0:T(1024)S(1)} %fusion.109), kind=kOutput, calls=%fused_computation.13 | convolution fusion | flops 8489533440 | bytes 54992896 | tf_op jit(solution)/shard_map/jvp()/dot_general | solution.py:457
  183.8 14.2 %fusion.34 = (f32[2048]{0:T(1024)S(1)}, bf16[2048,896]{0,1:T(8,128)(2,1)S(1)}) fusion(bf16[2048,2304]{1,0:T(8,128)(2,1)} %get-tuple-element.32, bf16[288,8,7,128]{3,2,1,0:T(8,128)(2,1)} %bitcast.204, bf16[1,2048,896]{1,2,0:T(8,128)(2,1)} %copy.41), kind=kOutput, calls=%fused_computation.58 | convolution fusion | flops 8464889856 | bytes 20914176 | tf_op jit(solution)/shard_map/jvp()/dot_general | solution.py:445
  198.7 13.8 %fusion.73 = f32[2048,2304]{1,0:T(8,128)} fusion(bf16[896,2304]{1,0:T(8,128)(2,1)S(1)} %bitcast.214, bf16[2048,896]{0,1:T(8,128)(2,1)S(1)} %get-tuple-element.35, f32[2048]{0:T(1024)S(1)} %fusion.110), kind=kOutput, calls=%fused_computation.96 | convolution fusion | flops 8461221888 | bytes 26681344 | tf_op jit(solution)/shard_map/jvp()/dot_general | solution.py:457
  212.4 25.3 %fusion.1 = (bf16[2048,2304]{1,0:T(8,128)(2,1)}, f32[2048,2304]{1,0:T(8,128)}) fusion(f32[2048,2304]{1,0:T(8,128)} %fusion.73, bf16[2304,2048]{0,1:T(8,128)(2,1)} %convolution_convert_fusion.1, bf16[896,2304]{1,0:T(8,128)(2,1)S(1)} %bitcast.211, bf16[2048,896]{0,1:T(8,128)(2,1)S(1)} %get-tuple-element.35, f32[2048]{0:T(1024)S(1)} %fusion.110), kind=kOutput, calls=%fused_computation.5 | convolution fusion | flops 8517844992 | bytes 64430080 | tf_op jit(solution)/shard_map/jvp()/dot_general | solution.py:456
  237.7 19.5 %fusion.37 = bf16[2304,896]{1,0:T(8,128)(2,1)} fusion(f32[2048,2304]{1,0:T(8,128)} %fusion.73, bf16[1,2048,896]{2,1,0:T(8,128)(2,1)} %param.18, f32[2048,2304]{1,0:T(8,128)} %get-tuple-element.37), kind=kOutput, calls=%fused_computation.62 | convolution fusion | flops 8486092800 | bytes 45547520 | tf_op jit(solution)/shard_map/transpose(jvp())/dot_general | solution.py:445
  257.2 17.4 %fusion.7 = bf16[2048,896]{0,1:T(8,128)(2,1)} fusion(bf16[896,2304]{1,0:T(8,128)(2,1)} %bitcast.213, bf16[2304,2048]{0,1:T(8,128)(2,1)} %convolution_convert_fusion.1, f32[2048,2304]{1,0:T(8,128)} %get-tuple-element.37), kind=kOutput, calls=%fused_computation.19 | convolution fusion | flops 8484028416 | bytes 36110336 | tf_op jit(solution)/shard_map/transpose(jvp())/dot_general | solution.py:457
  274.6 17.2 %fusion.39 = bf16[896,2304]{1,0:T(8,128)(2,1)} fusion(bf16[2304,2048]{0,1:T(8,128)(2,1)} %convolution_convert_fusion.1, bf16[2048,896]{0,1:T(8,128)(2,1)S(1)} %copy-done.19, f32[2048]{0:T(1024)S(1)} %fusion.110, f32[2048,2304]{1,0:T(8,128)} %get-tuple-element.37), kind=kOutput, calls=%fused_computation.64 | convolution fusion | flops 8491597824 | bytes 36118528 | tf_op jit(solution)/shard_map/transpose(jvp())/dot_general | solution.py:457
  291.8 12.5 %fusion.36 = (f32[2048]{0:T(1024)S(1)}, bf16[2048,896]{0,1:T(8,128)(2,1)S(1)}) fusion(bf16[2048,896]{0,1:T(8,128)(2,1)S(1)} %copy-done.19, bf16[2048,896]{0,1:T(8,128)(2,1)} %fusion.7, bf16[2048,2304]{1,0:T(8,128)(2,1)} %get-tuple-element.36, bf16[896,2304]{1,0:T(8,128)(2,1)S(1)} %bitcast.212), kind=kOutput, calls=%fused_computation.60 | convolution fusion | flops 8464889856 | bytes 24584192 | tf_op jit(solution)/shard_map/transpose(jvp())/dot_general | solution.py:456
  304.3 13.8 %convolution_convert_fusion.2 = bf16[896,2304]{1,0:T(8,128)(2,1)} fusion(bf16[2048,2304]{1,0:T(8,128)(2,1)} %get-tuple-element.36, bf16[2048,896]{0,1:T(8,128)(2,1)S(1)} %copy-done.19, f32[2048]{0:T(1024)S(1)} %fusion.110), kind=kOutput, calls=%fused_computation.65 | convolution fusion | flops 8461221888 | bytes 17244160 | tf_op jit(solution)/shard_map/transpose(jvp())/dot_general | solution.py:456
  322.9 14.1 %convolution_convert_fusion.3 = bf16[2304,896]{1,0:T(8,128)(2,1)} fusion(bf16[2048,2304]{1,0:T(8,128)(2,1)} %get-tuple-element.32, bf16[2048,896]{0,1:T(8,128)(2,1)S(1)} %fusion.52), kind=kOutput, calls=%fused_computation.66 | convolution fusion | flops 8457781248 | bytes 17235968 | tf_op jit(solution)/shard_map/transpose(jvp())/dot_general | solution.py:445
  337.1 31.0 %fusion.3 = (bf16[2048,2304]{1,0:T(8,128)(2,1)}, bf16[2048,2304]{1,0:T(8,128)(2,1)}) fusion(f32[2048,2304]{1,0:T(8,128)} %fusion.79, f32[2048,2304]{1,0:T(8,128)} %get-tuple-element.33, bf16[2048,896]{0,1:T(8,128)(2,1)} %copy-done.7, bf16[288,8,7,128]{3,2,1,0:T(8,128)(2,1)} %bitcast.205), kind=kOutput, calls=%fused_computation.7 | convolution fusion | flops 8517058560 | bytes 64421888 | tf_op jit(solution)/shard_map/transpose(jvp())/dot_general | solution.py:445
  368.1 17.3 %fusion.9 = bf16[2048,896]{0,1:T(8,128)(2,1)} fusion(bf16[896,2304]{1,0:T(8,128)(2,1)} %bitcast.210, bf16[2048,2304]{1,0:T(8,128)(2,1)} %get-tuple-element.41, f32[2048,2304]{1,0:T(8,128)} %fusion.79), kind=kOutput, calls=%fused_computation.21 | convolution fusion | flops 8484028416 | bytes 36110336 | tf_op jit(solution)/shard_map/transpose(jvp())/dot_general | solution.py:457
  385.4 17.1 %fusion.38 = bf16[896,2304]{1,0:T(8,128)(2,1)} fusion(bf16[2048,2304]{1,0:T(8,128)(2,1)} %get-tuple-element.41, bf16[1,2048,896]{1,2,0:T(8,128)(2,1)S(1)} %copy-done.1, f32[2048]{0:T(1024)S(1)} %copy-done.28, f32[2048,2304]{1,0:T(8,128)} %fusion.79), kind=kOutput, calls=%fused_computation.63 | convolution fusion | flops 8491597824 | bytes 36118528 | tf_op jit(solution)/shard_map/transpose(jvp())/dot_general | solution.py:457
  402.5 12.5 %fusion.32 = (f32[2048]{0:T(1024)S(1)}, bf16[2048,896]{0,1:T(8,128)(2,1)S(1)}) fusion(bf16[1,2048,896]{1,2,0:T(8,128)(2,1)S(1)} %copy-done.1, bf16[2048,896]{0,1:T(8,128)(2,1)} %fusion.9, bf16[2048,2304]{1,0:T(8,128)(2,1)} %get-tuple-element.40, bf16[896,2304]{1,0:T(8,128)(2,1)S(1)} %bitcast.208), kind=kOutput, calls=%fused_computation.56 | convolution fusion | flops 8464889856 | bytes 24584192 | tf_op jit(solution)/shard_map/transpose(jvp())/dot_general | solution.py:456
  415.0 13.7 %convolution_convert_fusion.4 = bf16[896,2304]{1,0:T(8,128)(2,1)} fusion(bf16[2048,2304]{1,0:T(8,128)(2,1)} %get-tuple-element.40, bf16[1,2048,896]{1,2,0:T(8,128)(2,1)S(1)} %copy-done.1, f32[2048]{0:T(1024)S(1)} %copy-done.28), kind=kOutput, calls=%fused_computation.67 | convolution fusion | flops 8461221888 | bytes 17244160 | tf_op jit(solution)/shard_map/transpose(jvp())/dot_general | solution.py:456
  433.4 6.1 copy.57
  439.5 8.1 %fusion.21 = bf16[8,2304,256]{1,2,0:T(8,128)(2,1)} fusion(bf16[224,256,1]{1,0,2:T(8,128)(2,1)S(1)} %copy-done.23, bf16[8,112,2304]{2,1,0:T(8,128)(2,1)} %bitcast.217, bf16[8,112,2304]{2,1,0:T(8,128)(2,1)} %bitcast.218), kind=kOutput, calls=%fused_computation.49 | convolution fusion | flops 2135162880 | bytes 17809408 | tf_op jit(solution)/shard_map/rk,grn->gkn/dot_general | solution.py:401
  447.9 5.5 fusion.24
  461.3 9.0 %reshape_reshape.6 = bf16[8,288,7,128]{3,2,1,0:T(8,128)(2,1)} reshape(bf16[2304,896]{1,0:T(8,128)(2,1)} %convolution_convert_fusion.3) | data formatting | bytes 8257536 | tf_op jit(solution)/shard_map/reshape;reshape | solution.py:440
  474.2 12.0 %pad_maximum_fusion.d = bf16[4,4,4,2,16,3328]{5,4,3,2,1,0:T(8,128)(2,1)} fusion(bf16[4,4,4,2,16,128]{5,4,3,2,1,0:T(8,128)(2,1)S(1)} %bitcast.215, bf16[4,4,4,2,16,896]{5,4,3,2,1,0:T(8,128)(2,1)} %bitcast.201, bf16[4,4,4,2,16,2304]{5,4,3,2,1,0:T(8,128)(2,1)} %bitcast.203), kind=kLoop, calls=%fused_computation.16 | loop fusion | flops 40894464 | bytes 27262976 | tf_op jit(solution)/shard_map/concatenate | solution.py:480
  486.2 47.5 %scatter.2 = bf16[16,3328]{1,0:T(8,128)(2,1)} custom-call(bf16[4,4,4,2,16,3328]{5,4,3,2,1,0:T(8,128)(2,1)} %pad_maximum_fusion.d), custom_call_target="tpu_custom_call" | custom-call | tf_op jit(solution)/shard_map/scatter/pallas_call | solution.py:373
  535.9 9.0 %reshape_reshape.7 = bf16[8,288,7,128]{3,2,1,0:T(8,128)(2,1)} reshape(bf16[2304,896]{1,0:T(8,128)(2,1)} %fusion.37) | data formatting | bytes 8257536 | tf_op jit(solution)/shard_map/reshape;reshape | solution.py:440
  548.9 12.0 %pad_maximum_fusion.1.d = bf16[4,4,4,2,16,3328]{5,4,3,2,1,0:T(8,128)(2,1)} fusion(bf16[4,4,4,2,16,128]{5,4,3,2,1,0:T(8,128)(2,1)S(1)} %bitcast.216, bf16[4,4,4,2,16,896]{5,4,3,2,1,0:T(8,128)(2,1)} %bitcast.200, bf16[4,4,4,2,16,2304]{5,4,3,2,1,0:T(8,128)(2,1)} %bitcast.202), kind=kLoop, calls=%fused_computation.17 | loop fusion | flops 40894464 | bytes 27262976 | tf_op jit(solution)/shard_map/concatenate | solution.py:480
  560.8 51.8 %scatter.3 = bf16[16,3328]{1,0:T(8,128)(2,1)} custom-call(bf16[4,4,4,2,16,3328]{5,4,3,2,1,0:T(8,128)(2,1)} %pad_maximum_fusion.1.d), custom_call_target="tpu_custom_call" | custom-call | tf_op jit(solution)/shard_map/scatter/pallas_call | solution.py:373
  (118 shorter events, 64.7 us)
Async XLA Ops:
  4.7 15.7 %copy-start.24 = (bf16[16,6656]{1,0:T(8,128)(2,1)}, bf16[16,6656]{1,0:T(8,128)(2,1)S(1)}, u32[]{:S(2)}) copy-start(bf16[16,6656]{1,0:T(8,128)(2,1)S(1)} %constant_dynamic-update-slice_fusion.shard) | copy-start | bytes 638980
  14.3 148.2 %copy-start.27 = (f32[2048]{0:T(1024)}, f32[2048]{0:T(1024)S(1)}, u32[]{:S(2)}) copy-start(f32[2048]{0:T(1024)S(1)} %fusion.109) | copy-start | bytes 24580
  99.3 7.3 %copy-start.22 = (bf16[224,256,1]{1,0,2:T(8,128)(2,1)S(1)}, bf16[224,256,1]{1,0,2:T(8,128)(2,1)}, u32[]{:S(2)}) copy-start(bf16[224,256,1]{1,0,2:T(8,128)(2,1)} %constant.49) | copy-start | bytes 344068
  114.5 6.3 %copy-start = (bf16[8,224,2304]{2,1,0:T(8,128)(2,1)S(1)}, bf16[8,224,2304]{2,1,0:T(8,128)(2,1)}, u32[]{:S(2)}) copy-start(bf16[8,224,2304]{2,1,0:T(8,128)(2,1)} %convert_bitcast_fusion) | copy-start | bytes 24772612
  120.7 4.7 copy-start.3
  120.7 4.7 copy-start.20
  125.4 1.3 copy-start.14
  128.0 4.0 copy-start.2
  134.7 2.0 copy-start.17
  136.7 12.3 %copy-start.9 = (bf16[8,112,2304]{2,1,0:T(8,128)(2,1)S(1)}, bf16[8,112,2304]{2,1,0:T(8,128)(2,1)}, u32[]{:S(2)}) copy-start(bf16[8,112,2304]{2,1,0:T(8,128)(2,1)} %get-tuple-element.20) | copy-start | bytes 12386308
  136.7 12.3 %copy-start.16 = (bf16[1,2048,896]{2,1,0:T(8,128)(2,1)S(1)}, bf16[1,2048,896]{2,1,0:T(8,128)(2,1)}, u32[]{:S(2)}) copy-start(bf16[1,2048,896]{2,1,0:T(8,128)(2,1)} %param.17) | copy-start | bytes 11010052
  183.8 14.8 %copy-start.13 = (bf16[8,112,2304]{2,1,0:T(8,128)(2,1)S(1)}, bf16[8,112,2304]{2,1,0:T(8,128)(2,1)}, u32[]{:S(2)}) copy-start(bf16[8,112,2304]{2,1,0:T(8,128)(2,1)} %get-tuple-element.19) | copy-start | bytes 12386308
  198.0 0.6 copy-start.29
  198.1 14.4 %copy-start.18 = (bf16[2048,896]{0,1:T(8,128)(2,1)}, bf16[2048,896]{0,1:T(8,128)(2,1)S(1)}, u32[]{:S(2)}) copy-start(bf16[2048,896]{0,1:T(8,128)(2,1)S(1)} %get-tuple-element.35) | copy-start | bytes 11010052
  198.7 13.8 %copy-start.11 = (bf16[8,112,2304]{2,1,0:T(8,128)(2,1)S(1)}, bf16[8,112,2304]{2,1,0:T(8,128)(2,1)}, u32[]{:S(2)}) copy-start(bf16[8,112,2304]{2,1,0:T(8,128)(2,1)} %get-tuple-element.18) | copy-start | bytes 12386308
  257.2 17.4 %copy-start.19 = (bf16[2048,896]{0,1:T(8,128)(2,1)S(1)}, bf16[2048,896]{0,1:T(8,128)(2,1)}, u32[]{:S(2)}) copy-start(bf16[2048,896]{0,1:T(8,128)(2,1)} %copy-done.18) | copy-start | bytes 11010052
  274.6 17.2 %copy-start.12 = (bf16[8,112,2304]{2,1,0:T(8,128)(2,1)S(1)}, bf16[8,112,2304]{2,1,0:T(8,128)(2,1)}, u32[]{:S(2)}) copy-start(bf16[8,112,2304]{2,1,0:T(8,128)(2,1)} %get-tuple-element.18) | copy-start | bytes 12386308
  304.3 13.8 %copy-start.30 = (f32[2048]{0:T(1024)S(1)}, f32[2048]{0:T(1024)}, u32[]{:S(2)}) copy-start(f32[2048]{0:T(1024)} %copy-done.29) | copy-start | bytes 24580
  304.3 13.8 %copy-start.6 = (bf16[1,2048,896]{1,2,0:T(8,128)(2,1)S(1)}, bf16[1,2048,896]{1,2,0:T(8,128)(2,1)}, u32[]{:S(2)}) copy-start(bf16[1,2048,896]{1,2,0:T(8,128)(2,1)} %copy.40) | copy-start | bytes 11010052
  321.1 1.8 copy-start.7
  368.1 17.3 %copy-start.1 = (bf16[1,2048,896]{1,2,0:T(8,128)(2,1)S(1)}, bf16[1,2048,896]{1,2,0:T(8,128)(2,1)}, u32[]{:S(2)}) copy-start(bf16[1,2048,896]{1,2,0:T(8,128)(2,1)} %copy.41) | copy-start | bytes 11010052
  368.1 17.3 %copy-start.28 = (f32[2048]{0:T(1024)S(1)}, f32[2048]{0:T(1024)}, u32[]{:S(2)}) copy-start(f32[2048]{0:T(1024)} %copy-done.27) | copy-start | bytes 24580
  385.4 17.1 %copy-start.10 = (bf16[8,112,2304]{2,1,0:T(8,128)(2,1)S(1)}, bf16[8,112,2304]{2,1,0:T(8,128)(2,1)}, u32[]{:S(2)}) copy-start(bf16[8,112,2304]{2,1,0:T(8,128)(2,1)} %get-tuple-element.20) | copy-start | bytes 12386308
  415.0 13.8 %copy-start.26 = (f32[2048]{0:T(1024)S(1)}, f32[2048]{0:T(1024)}, u32[]{:S(2)}) copy-start(f32[2048]{0:T(1024)} %copy-done.25) | copy-start | bytes 24580
  415.0 13.8 %copy-start.8 = (bf16[2048,896]{0,1:T(8,128)(2,1)S(1)}, bf16[2048,896]{0,1:T(8,128)(2,1)}, u32[]{:S(2)}) copy-start(bf16[2048,896]{0,1:T(8,128)(2,1)} %copy-done.7) | copy-start | bytes 11010052
  433.4 6.1 copy-start.23
  439.5 8.1 %copy-start.31 = (bf16[896,2304]{1,0:T(8,128)(2,1)S(1)}, bf16[896,2304]{1,0:T(8,128)(2,1)}, u32[]{:S(2)}) copy-start(bf16[896,2304]{1,0:T(8,128)(2,1)} %fusion.38) | copy-start | bytes 12386308
  439.5 8.4 %copy-start.32 = (bf16[896,2304]{1,0:T(8,128)(2,1)S(1)}, bf16[896,2304]{1,0:T(8,128)(2,1)}, u32[]{:S(2)}) copy-start(bf16[896,2304]{1,0:T(8,128)(2,1)} %convolution_convert_fusion.4) | copy-start | bytes 12386308
  447.9 5.5 copy-start.4
  447.9 5.5 copy-start.21
  453.4 4.0 copy-start.5
  457.3 12.9 %copy-start.15 = (bf16[7,288,256,1]{2,1,0,3:T(8,128)(2,1)S(1)}, bf16[7,288,256,1]{2,1,0,3:T(8,128)(2,1)}, u32[]{:S(2)}) copy-start(bf16[7,288,256,1]{2,1,0,3:T(8,128)(2,1)} %constant.51) | copy-start | bytes 3096580
  (1 other events, 0.6 us)

commit v2 on v1

--- a/solution.py
+++ b/solution.py
@@ -68,33 +68,35 @@
         self.xyz, self.c = where()
         self.pending, self.partner = [], []
 
-    def block(self, k, phase, xyz, half):
-        order = ORDERS[k]
+    def at(self, k, phase, by):
+        return moved(self.xyz, ORDERS[k][phase], by)
+
+    def block(self, k, phase, by, half, c):
+        order, xyz = ORDERS[k], self.at(k, phase, by)
         at = [slice(None) if axis in order[:phase] else xyz[axis] for axis in range(3)]
         start, size = self.cols[k][half]
-        return self.g.at[at[0], at[1], at[2], self.c, :, pl.ds(start, size)]
-
-    def copy(self, k, phase, owner, half, to, slot, first=False):
-        here = self.block(k, phase, owner, half)
+        return self.g.at[at[0], at[1], at[2], c, :, pl.ds(start, size)]
+
+    def copy(self, k, phase, owner, half, to, slot):
+        here = self.block(k, phase, owner, half, self.c)
         start, size = self.cols[k][half]
-        src = self.shard.at[:, pl.ds(start, size)] if first else here
-        return remote(src, here, self.send.at[k, phase, slot], self.recv.at[k, phase, slot], to, self.c)
+        src = self.shard.at[:, pl.ds(start, size)] if phase == 0 and owner == 0 else here
+        return remote(src, here, self.send.at[k, phase, slot], self.recv.at[k, phase, slot], self.at(k, phase, to), self.c)
 
     def local(self):
         return pltpu.make_async_copy(self.shard, self.g.at[self.xyz[0], self.xyz[1], self.xyz[2], self.c], self.lsem)
 
-    def give(self, k, phase, owner, half, slot):
-        here = self.block(k, phase, owner, half)
-        copy = remote(here, here, self.dsend.at[k, slot], self.drecv.at[k, slot], self.xyz, 1 - self.c)
-        copy.start()
-        there = self.block_of_partner(k, phase, owner, half)
-        self.partner.append((copy, remote(there, there, self.dsend.at[k, slot], self.drecv.at[k, slot], self.xyz, 1 - self.c)))
-
-    def block_of_partner(self, k, phase, owner, half):
-        order = ORDERS[k]
-        at = [slice(None) if axis in order[:phase] else owner[axis] for axis in range(3)]
-        start, size = self.cols[k][half]
-        return self.g.at[at[0], at[1], at[2], 1 - self.c, :, pl.ds(start, size)]
+    def over(self, k, phase, owner, half, slot, c):
+        here = self.block(k, phase, owner, half, c)
+        return remote(here, here, self.dsend.at[k, slot], self.drecv.at[k, slot], self.xyz, 1 - self.c)
+
+    def go(self, *what):
+        self.copy(*what).start()
+        self.pending.append(what)
+
+    def give(self, *what):
+        self.over(*what, self.c).start()
+        self.partner.append(what)
 
     def begin(self, phase):
         if phase == 0:
@@ -102,49 +104,43 @@
         if phase == 1:
             self.local().wait()
         for k in range(3):
-            axis = ORDERS[k][phase]
-            right, left = moved(self.xyz, axis, 1), moved(self.xyz, axis, -1)
-            for to, half, slot in ((right, 0, 0), (left, 1, 3), (right, 1, 1), (left, 0, 2)):
-                copy = self.copy(k, phase, self.xyz, half, to, slot, phase == 0)
-                copy.start()
-                self.pending.append(copy)
+            for to, half, slot in ((1, 0, 0), (-1, 1, 3), (1, 1, 1), (-1, 0, 2)):
+                self.go(k, phase, 0, half, to, slot)
             if phase == 2:
                 for half in range(2):
-                    self.give(k, 2, self.xyz, half, half)
+                    self.give(k, 2, 0, half, half)
 
     def relay(self, phase):
         for k in range(3):
-            axis = ORDERS[k][phase]
-            right, left = moved(self.xyz, axis, 1), moved(self.xyz, axis, -1)
-            for owner, to, half, slot, out in ((left, right, 0, 0, 4), (right, left, 1, 3, 5)):
+            for owner, to, half, slot, out in ((-1, 1, 0, 0, 4), (1, -1, 1, 3, 5)):
                 self.copy(k, phase, owner, half, to, slot).wait_recv()
-                copy = self.copy(k, phase, owner, half, to, out)
-                copy.start()
-                self.pending.append(copy)
+                self.go(k, phase, owner, half, to, out)
                 if phase == 2:
                     self.give(k, 2, owner, half, 2 + half)
 
     def finish(self, phase):
         for k in range(3):
-            axis = ORDERS[k][phase]
-            right, left, far = moved(self.xyz, axis, 1), moved(self.xyz, axis, -1), moved(self.xyz, axis, 2)
-            for owner, half, slot, give in ((left, 1, 1, 4), (right, 0, 2, 5), (far, 0, 4, 6), (far, 1, 5, 7)):
-                self.copy(k, phase, owner, half, owner, slot).wait_recv()
+            for owner, half, slot, give in ((-1, 1, 1, 4), (1, 0, 2, 5), (2, 0, 4, 6), (2, 1, 5, 7)):
+                self.copy(k, phase, owner, half, 1, slot).wait_recv()
                 if phase == 2:
                     self.give(k, 2, owner, half, give)
 
     def end(self):
-        for mine, theirs in self.partner:
-            theirs.wait_recv()
-            mine.wait_send()
-        for copy in self.pending:
-            copy.wait_send()
+        for what in self.partner:
+            self.over(*what, 1 - self.c).wait_recv()
+            self.over(*what, self.c).wait_send()
+        for what in self.pending:
+            self.copy(*what).wait_send()
 
     def steps(self):
-        out = []
-        for phase in range(3):
-            out += [functools.partial(f, phase) for f in (self.begin, self.relay, self.finish)]
-        return out + [self.end]
+        out = [functools.partial(self.begin, 0), functools.partial(self.relay, 0)]
+        for phase in (1, 2):
+            out += [functools.partial(self.turn, phase), functools.partial(self.relay, phase)]
+        return out + [functools.partial(self.finish, 2), self.end]
+
+    def turn(self, phase):
+        self.finish(phase - 1)
+        self.begin(phase)
 
 
 GATHER_SEMS = [
@@ -242,26 +238,22 @@
         return self.own if phase == 0 else self.next[phase - 1]
 
     def copy(self, k, phase, half, slot, to, to_at, dst):
-        src = self.buf(phase).at[(*self.source(k, phase, to_at), slice(None), self.cut(k, half))]
+        axis = ORDERS[k][phase]
+        at, to = moved(self.xyz, axis, to_at)[axis], moved(self.xyz, axis, to)
+        src = self.buf(phase).at[(*self.source(k, phase, at), slice(None), self.cut(k, half))]
         lead = [slice(None)] * (2 - phase)
         there = dst[phase].at[(*lead, slice(None), self.cut(k, half))]
         return remote(src, there, self.send.at[k, phase, slot], self.recv.at[k, phase, slot], to, self.c)
 
-    def sides(self, k, phase):
-        axis = ORDERS[k][phase]
-        right, left = moved(self.xyz, axis, 1), moved(self.xyz, axis, -1)
-        return right, left, right[axis], left[axis], lax.rem(self.xyz[axis] + 2, 4)
+    def go(self, *what):
+        self.copy(*what).start()
+        self.pending.append(what)
 
     def first(self, k, phase):
-        right, left, ri, li, far = self.sides(k, phase)
-        for copy in (
-            self.copy(k, phase, 0, 0, right, far, self.one),
-            self.copy(k, phase, 1, 1, left, far, self.one),
-            self.copy(k, phase, 1, 2, right, ri, self.l2),
-            self.copy(k, phase, 0, 3, left, li, self.r2),
-        ):
-            copy.start()
-            self.pending.append(copy)
+        self.go(k, phase, 0, 0, 1, 2, self.one)
+        self.go(k, phase, 1, 1, -1, 2, self.one)
+        self.go(k, phase, 1, 2, 1, 1, self.l2)
+        self.go(k, phase, 0, 3, -1, -1, self.r2)
 
     def shards(self, phase):
         return (16, 4, 1)[phase]
@@ -270,11 +262,11 @@
         return ((i // 4, lax.rem(i, 4)), (i,), ())[phase]
 
     def second(self, k, phase):
-        right, left, ri, li, far = self.sides(k, phase)
-        for half, slot, to, to_at, dst, out in ((0, 0, right, ri, self.l2, 4), (1, 1, left, li, self.r2, 5)):
-            self.copy(k, phase, half, slot, to, far, self.one).wait_recv()
+        axis = ORDERS[k][phase]
+        for half, slot, to, dst, out in ((0, 0, 1, self.l2, 4), (1, 1, -1, self.r2, 5)):
+            self.copy(k, phase, half, slot, to, 2, self.one).wait_recv()
             at, buf = self.cut(k, half), self.buf(phase)
-            where_ = self.source(k, phase, to_at)
+            where_ = self.source(k, phase, moved(self.xyz, axis, to)[axis])
 
             def body(i, _):
                 lead = self.lead(phase, i)
@@ -286,14 +278,11 @@
                 return 0
 
             lax.fori_loop(0, self.shards(phase), body, 0)
-            copy = self.copy(k, phase, half, out, to, to_at, dst)
-            copy.start()
-            self.pending.append(copy)
+            self.go(k, phase, half, out, to, to, dst)
 
     def third(self, k, phase):
-        right, left, ri, li, far = self.sides(k, phase)
         for half, slot, dst in ((1, 2, self.l2), (0, 3, self.r2), (0, 4, self.l2), (1, 5, self.r2)):
-            self.copy(k, phase, half, slot, right, ri, dst).wait_recv()
+            self.copy(k, phase, half, slot, 1, 1, dst).wait_recv()
         at, order = self.both(k), ORDERS[k]
 
         def body(i, _):
@@ -322,19 +311,27 @@
     def end(self):
         for k in range(3):
             self.swap(k).wait_send()
-        for copy in self.pending:
-            copy.wait_send()
+        for what in self.pending:
+            self.copy(*what).wait_send()
+
+    def opened(self, k):
+        self.add_swap(k)
+        self.first(k, 0)
+
+    def seconds(self, phase):
+        for k in range(3):
+            self.second(k, phase)
+
+    def thirds(self, phase):
+        for k in range(3):
+            self.third(k, phase)
+            if phase < 2:
+                self.first(k, phase + 1)
 
     def steps(self):
-        out = [self.begin_swap]
-        for k in range(3):
-            out += [functools.partial(self.add_swap, k), functools.partial(self.first, k, 0)]
+        out = [self.begin_swap, *[functools.partial(self.opened, k) for k in range(3)]]
         for phase in range(3):
-            out += [functools.partial(self.second, k, phase) for k in range(3)]
-            for k in range(3):
-                out.append(functools.partial(self.third, k, phase))
-                if phase < 2:
-                    out.append(functools.partial(self.first, k, phase + 1))
+            out += [functools.partial(self.seconds, phase), functools.partial(self.thirds, phase)]
         return out + [self.end]
 
 
@@ -414,75 +411,235 @@
     return gate, up, down
 
 
-def unpack_gu(g):
-    gu = picks()[0]
-    w = one_hot("rk,gkn->grn", gu, g.reshape(8, 256, FF)).astype(BF)
-    return w[:, :112].reshape(D, FF), w[:, 112:].reshape(D, FF)
-
-
-def unpack_down(g):
-    _, main, extra = picks()
-    g = g.reshape(8, 256, 1024)
-    w = one_hot("rk,gkn->grn", main, g[..., :D]).reshape(8, 288, 7, 128) + one_hot("trk,gkn->grtn", extra, g[..., D:])
-    return w.astype(BF).reshape(FF, D)
-
-
-def pack_gu(gate, up):
-    gu = picks()[0]
-    w = jnp.concatenate([gate.reshape(8, 112, FF), up.reshape(8, 112, FF)], 1)
-    return one_hot("rk,grn->gkn", gu, w).astype(BF).reshape(4, 4, 4, 2, 16, FF)
-
-
-def pack_down(down):
-    _, main, extra = picks()
-    w = down.reshape(8, 288, D)
-    a = one_hot("rk,grn->gkn", main, w)
-    b = one_hot("trk,grtn->gkn", extra, w.reshape(8, 288, 7, 128))
-    return jnp.concatenate([a, b], -1).astype(BF).reshape(4, 4, 4, 2, 16, 1024)
-
-
-def matmul(a, w):
-    return jnp.dot(a, w, preferred_element_type=F32).astype(BF)
-
-
-def normed(h):
+def unpack_kernel(g, gu, main, extra, wg, wu, wd):
+    both = one_hot("rk,kn->rn", gu[...], g[0, :, :FF]).astype(BF)
+    wg[...] = both[:112]
+    wu[...] = both[112:]
+    first = one_hot("rk,kn->rn", main[...], g[0, :, FF : FF + D])
+    for t in range(7):
+        at = slice(128 * t, 128 * t + 128)
+        wd[:, at] = (first[:, at] + one_hot("rk,kn->rn", extra[t], g[0, :, FF + D :])).astype(BF)
+
+
+def whole(shape):
+    return pl.BlockSpec(shape, lambda i: (0,) * len(shape), pipeline_mode=pl.Buffered(1))
+
+
+def rows(n, width):
+    return pl.BlockSpec((n, width), lambda i: (i, 0))
+
+
+def like(n, width, dtype=BF):
+    return jax.ShapeDtypeStruct((n, width), dtype)
+
+
+def params(**more):
+    return pltpu.CompilerParams(dimension_semantics=("arbitrary",), vmem_limit_bytes=62 * 2**20, **more)
+
+
+PICKS = [whole((224, 256)), whole((288, 256)), whole((7, 288, 256))]
+
+
+def unpack(g):
+    return pl.pallas_call(
+        unpack_kernel,
+        grid=(8,),
+        in_specs=[pl.BlockSpec((1, 256, C), lambda i: (i, 0, 0)), *PICKS],
+        out_specs=[rows(112, FF), rows(112, FF), rows(288, D)],
+        out_shape=[like(D, FF), like(D, FF), like(FF, D)],
+        compiler_params=params(),
+        name="unpack",
+    )(g.reshape(8, 256, C), *picks())
+
+
+def pack_kernel(dg, du, dd, gu, main, extra, out):
+    both = jnp.concatenate([dg[...], du[...]], 0)
+    out[0, :, :FF] = one_hot("rk,rn->kn", gu[...], both).astype(BF)
+    out[0, :, FF : FF + D] = one_hot("rk,rn->kn", main[...], dd[...]).astype(BF)
+    last = jnp.zeros((256, 128), F32)
+    for t in range(7):
+        last += one_hot("rk,rn->kn", extra[t], dd[:, 128 * t : 128 * t + 128])
+    out[0, :, FF + D :] = last.astype(BF)
+
+
+def pack(dg, du, dd):
+    out = pl.pallas_call(
+        pack_kernel,
+        grid=(8,),
+        in_specs=[rows(112, FF), rows(112, FF), rows(288, D), *PICKS],
+        out_specs=pl.BlockSpec((1, 256, C), lambda i: (i, 0, 0)),
+        out_shape=jax.ShapeDtypeStruct((8, 256, C), BF),
+        compiler_params=params(),
+        name="pack",
+    )(dg, du, dd, *picks())
+    return out.reshape(4, 4, 4, 2, 16, C)
+
+
+CHUNK = 768
+CHUNKS = tuple(slice(at, at + CHUNK) for at in range(0, FF, CHUNK))
+
+
+def mm(a, w):
+    return lax.dot_general(a, w, (((1,), (0,)), ((), ())), preferred_element_type=F32)
+
+
+def mmt(a, w):
+    return lax.dot_general(a, w, (((1,), (1,)), ((), ())), preferred_element_type=F32)
+
+
+def norm(h):
     wide = h.astype(F32)
-    scale = lax.rsqrt(jnp.mean(wide**2, -1, keepdims=True) + 1e-6)
-    return (wide * scale).astype(BF)
-
-
-def layer(h, w):
-    a = normed(h)
-    gate = jnp.dot(a, w[0], preferred_element_type=F32)
-    up = jnp.dot(a, w[1], preferred_element_type=F32)
-    return h + matmul((jax.nn.silu(gate) * up).astype(BF), w[2])
-
-
-def stack(weights, h):
-    for w in weights:
-        h = layer(h, w)
-    return h
+    scale = lax.rsqrt(jnp.mean(wide * wide, -1, keepdims=True) + 1e-6)
+    return wide, scale
+
+
+def norm_back(wide, scale, da, dh):
+    da = da.astype(BF).astype(F32)
+    inner = jnp.mean(da * wide, -1, keepdims=True)
+    by_h = (da * scale - wide * (scale * scale * scale * inner)).astype(BF)
+    return (dh.astype(F32) + by_h.astype(F32)).astype(BF)
+
+
+def gate_back(g, u, ds):
+    sig = 1.0 / (1.0 + jnp.exp(-g))
+    soft = g * sig
+    du = (ds * soft).astype(BF)
+    dg = (ds * u * (sig * (1.0 + g - soft))).astype(BF)
+    return soft, dg, du
+
+
+def at_step(number, step):
+    @pl.when(pl.program_id(0) == number)
+    def _():
+        step()
+
+
+def forward_kernel(x, wg, wu, wd, shard, h, a_out, g_out, u_out, s_out, gathered, *sems):
+    gather = Gather(colours(0, C), shard, gathered, *sems)
+    steps = gather.steps()
+
+    def start():
+        rendezvous(gather.xyz, gather.c)
+        steps[0]()
+
+    at_step(0, start)
+    for n, step in enumerate(steps[1:-1]):
+        at_step(n + 1, step)
+    wide, scale = norm(x[...])
+    a = (wide * scale).astype(BF)
+    a_out[...] = a
+    for at in CHUNKS:
+        g, u = mm(a, wg[:, at]), mm(a, wu[:, at])
+        g_out[:, at] = g
+        u_out[:, at] = u
+        s_out[:, at] = (g * (1.0 / (1.0 + jnp.exp(-g))) * u).astype(BF)
+    h[...] = (x[...].astype(F32) + mm(s_out[...], wd[...]).astype(BF).astype(F32)).astype(BF)
+    at_step(7, steps[-1])
+
+
+def forward(x, weights, shard):
+    n = TOK // 8
+    return pl.pallas_call(
+        forward_kernel,
+        grid=(8,),
+        in_specs=[rows(n, D), whole((D, FF)), whole((D, FF)), whole((FF, D)), whole((16, C))],
+        out_specs=[rows(n, D), rows(n, D), rows(n, FF), rows(n, FF), rows(n, FF), ANY],
+        out_shape=[
+            like(TOK, D), like(TOK, D), like(TOK, FF, F32), like(TOK, FF, F32), like(TOK, FF),
+            jax.ShapeDtypeStruct((4, 4, 4, 2, 16, C), BF),
+        ],
+        scratch_shapes=GATHER_SEMS,
+        compiler_params=params(collective_id=2, has_side_effects=True),
+        name="forward",
+    )(x, *weights, shard)
+
+
+def middle_kernel(h, dy, wg, wu, wd, a_out, s_out, dg_out, du_out, dh):
+    wide, scale = norm(h[...])
+    a = (wide * scale).astype(BF)
+    a_out[...] = a
+    da = None
+    for at in CHUNKS:
+        g, u = mm(a, wg[:, at]), mm(a, wu[:, at])
+        ds = mmt(dy[...], wd[at, :]).astype(BF).astype(F32)
+        soft, dg, du = gate_back(g, u, ds)
+        s_out[:, at] = (soft * u).astype(BF)
+        dg_out[:, at] = dg
+        du_out[:, at] = du
+    da = mmt(dg_out[...], wg[...]) + mmt(du_out[...], wu[...])
+    dh[...] = norm_back(wide, scale, da, dy[...])
+
+
+def middle(h, dy, weights):
+    n = TOK // 4
+    return pl.pallas_call(
+        middle_kernel,
+        grid=(4,),
+        in_specs=[rows(n, D), rows(n, D), whole((D, FF)), whole((D, FF)), whole((FF, D))],
+        out_specs=[rows(n, D), rows(n, FF), rows(n, FF), rows(n, FF), rows(n, D)],
+        out_shape=[like(TOK, D), like(TOK, FF), like(TOK, FF), like(TOK, FF), like(TOK, D)],
+        compiler_params=params(),
+        name="middle",
+    )(h, dy, *weights)
+
+
+def backward_kernel(x, dh, g_in, u_in, wg, wu, wd, d, dg_out, du_out, dx, summed, *scratch):
+    scatter = make_scatter(colours(0, C), d, summed, scratch)
+    steps = scatter.steps()
+
+    def start():
+        rendezvous(scatter.xyz, scatter.c)
+        steps[0]()
+
+    at_step(0, start)
+    when = {3: (1, 2), 4: (3,), 6: (4,)}
+    for number, group in when.items():
+        for n in group:
+            at_step(number, steps[n])
+    for at in CHUNKS:
+        ds = mmt(dh[...], wd[at, :]).astype(BF).astype(F32)
+        _, dg, du = gate_back(g_in[:, at], u_in[:, at], ds)
+        dg_out[:, at] = dg
+        du_out[:, at] = du
+    wide, scale = norm(x[...])
+    da = mmt(dg_out[...], wg[...]) + mmt(du_out[...], wu[...])
+    dx[...] = norm_back(wide, scale, da, dh[...])
+    for step in steps[5:]:
+        at_step(7, step)
+
+
+def backward(x, dh, g, u, weights, d):
+    n = TOK // 8
+    return pl.pallas_call(
+        backward_kernel,
+        grid=(8,),
+        in_specs=[rows(n, D), rows(n, D), rows(n, FF), rows(n, FF), whole((D, FF)), whole((D, FF)), whole((FF, D)), ANY],
+        out_specs=[rows(n, FF), rows(n, FF), rows(n, D), pl.BlockSpec((16, C), lambda i: (0, 0))],
+        out_shape=[like(TOK, FF), like(TOK, FF), like(TOK, D), like(16, C)],
+        scratch_shapes=scatter_scratch(C),
+        compiler_params=params(collective_id=3, has_side_effects=True),
+        name="backward",
+    )(x, dh, g, u, *weights, d)
+
+
+def turned(a, b):
+    return lax.dot_general(a, b, (((0,), (0,)), ((), ())), preferred_element_type=F32).astype(BF)
 
 
 def solution(mesh):
     def step(x, dy, gate, up, down):
-        shard = jnp.concatenate([pack_shard(gate[n], up[n], down[n]) for n in range(2)], 1)
-        g = gather_call(shard, 0)
-        weights = []
-        for n in range(2):
-            part = g[..., n * C : (n + 1) * C]
-            weights.append((*unpack_gu(part[..., :FF]), unpack_down(part[..., FF:])))
-        _, back = jax.vjp(stack, weights, x[0])
-        by_weights, by_x = back(dy[0])
-        outs = []
-        for n in (1, 0):
-            dg, du, dd = by_weights[n]
-            d = jnp.concatenate([pack_gu(dg, du), pack_down(dd)], -1)
-            outs.append(unpack_shard(scatter_call(d, 1)))
-        outs = outs[::-1]
-        return (by_x[None], *(jnp.stack([o[i] for o in outs]) for i in range(3)))
-
-    rows = P(None, "dp", None)
+        x, dy = x[0], dy[0]
+        shards = [pack_shard(gate[n], up[n], down[n]) for n in range(2)]
+        w0 = unpack(gather_call(shards[0], 0))
+        h, a0, g0, u0, s0, g1 = forward(x, w0, shards[1])
+        a1, s1, dg1, du1, dh = middle(h, dy, unpack(g1))
+        d1 = pack(turned(a1, dg1), turned(a1, du1), turned(s1, dy))
+        dg0, du0, dx, sum1 = backward(x, dh, g0, u0, w0, d1)
+        d0 = pack(turned(a0, dg0), turned(a0, du0), turned(s0, dh))
+        outs = [unpack_shard(scatter_call(d0, 1)), unpack_shard(sum1)]
+        return (dx[None], *(jnp.stack([o[i] for o in outs]) for i in range(3)))
+
+    cut = P(None, "dp", None)
     return jax.shard_map(
-        step, mesh=mesh, in_specs=(P("dp"), P("dp"), rows, rows, rows), out_specs=(P("dp"), rows, rows, rows), check_vma=False
+        step, mesh=mesh, in_specs=(P("dp"), P("dp"), cut, cut, cut), out_specs=(P("dp"), cut, cut, cut), check_vma=False
     )

time: 629 us -> 451 us (0.72)
  the two profiles are of different devices: /device:TPU:17 before, /device:TPU:0 now
where the time goes in v2:
time: 451 us; the launch traced here: 443 us
  Pallas kernels  349 us (77%)
  matrix products  76.6 us (17%)
  local copies, waits for them, and re-layouts  14.7 us (3%)
    dot_general x6, matrix products, turned(): lax.dot_general(a, b, (((0,), (0,)), ((), ())), preferred_element_type=F32)  76.6 us
    pallas_call x1, Pallas kernels, backward(): pl.pallas_call(backward_kernel, grid=(8,), in_specs=[rows(n, D), rows(n,...  72.6 us
    pallas_call x1, Pallas kernels, middle(): pl.pallas_call(middle_kernel, grid=(4,), in_specs=[rows(n, D), rows(n, D)...  61.6 us
    pallas_call x1, Pallas kernels, forward(): pl.pallas_call(forward_kernel, grid=(8,), in_specs=[rows(n, D), whole((D,...  59.2 us
    pallas_call x1, Pallas kernels, scatter_call(): pl.pallas_call(functools.partial(scatter_kernel, colours(0, width)), out_...  50.1 us
    pallas_call x1, Pallas kernels, gather_call(): pl.pallas_call(functools.partial(gather_kernel, colours(0, width)), out_s...  48.4 us
    pallas_call x2, Pallas kernels, pack(): pl.pallas_call(pack_kernel, grid=(8,), in_specs=[rows(112, FF), rows(112,...  30.3 us
    pallas_call x2, Pallas kernels, unpack(): pl.pallas_call(unpack_kernel, grid=(8,), in_specs=[pl.BlockSpec((1, 256,...  27.3 us

profile of v2, /device:TPU:0, one launch (start us, length us, event | category | flops | bytes accessed | tf_op | source)
XLA Modules:
  0.0 443.4 jit_solution(8972268821237891988)
XLA Ops:
  0.6 0.8 slice_reduce_fusion
  1.5 1.0 fusion.19
  2.5 1.0 fusion.20
  3.6 1.0 fusion.21
  4.6 0.7 fusion.17.shard
  5.3 0.7 fusion.14.shard
  5.9 48.4 %gather.1 = bf16[4,4,4,2,16,3328]{5,4,3,2,1,0:T(8,128)(2,1)} custom-call(bf16[16,3328]{1,0:T(8,128)(2,1)} %fusion.14.shard), custom_call_target="tpu_custom_call" | custom-call | tf_op jit(solution)/shard_map/gather/pallas_call | solution.py:164
  54.3 13.7 %unpack.2 = (bf16[896,2304]{1,0:T(8,128)(2,1)}, bf16[896,2304]{1,0:T(8,128)(2,1)}, bf16[2304,896]{1,0:T(8,128)(2,1)}) custom-call(bf16[8,256,3328]{2,1,0:T(8,128)(2,1)} %bitcast.46, bf16[224,256]{1,0:T(8,128)(2,1)} %constant.9.clone.gu, bf16[288,256]{1,0:T(8,128)(2,1)} %constant.10.clone.main, bf16[7,288,256]{2,1,0:T(8,128)(2,1)} %constant.11.clone.extra), custom_call_target="tpu_custom_call" | custom-call | tf_op jit(solution)/shard_map/unpack/pallas_call | solution.py:444
  68.0 59.2 %forward.1 = (bf16[2048,896]{1,0:T(8,128)(2,1)}, bf16[2048,896]{1,0:T(8,128)(2,1)}, f32[2048,2304]{1,0:T(8,128)}, f32[2048,2304]{1,0:T(8,128)}, bf16[2048,2304]{...) custom-call(bf16[2048,896]{1,0:T(8,128)(2,1)} %bitcast.47, bf16[896,2304]{1,0:T(8,128)(2,1)} %get-tuple-element.25.wg, ...), custom_call_target="tpu_custom_call" | custom-call | tf_op jit(solution)/shard_map/forward/pallas_call | solution.py:542
  127.2 13.6 %unpack.3 = (bf16[896,2304]{1,0:T(8,128)(2,1)}, bf16[896,2304]{1,0:T(8,128)(2,1)}, bf16[2304,896]{1,0:T(8,128)(2,1)}) custom-call(bf16[8,256,3328]{2,1,0:T(8,128)(2,1)} %bitcast.49, bf16[224,256]{1,0:T(8,128)(2,1)} %constant.9.clone.gu, bf16[288,256]{1,0:T(8,128)(2,1)} %constant.10.clone.main, bf16[7,288,256]{2,1,0:T(8,128)(2,1)} %constant.11.clone.extra), custom_call_target="tpu_custom_call" | custom-call | tf_op jit(solution)/shard_map/unpack/pallas_call | solution.py:444
  140.8 61.6 %middle.1 = (bf16[2048,896]{1,0:T(8,128)(2,1)}, bf16[2048,2304]{1,0:T(8,128)(2,1)}, bf16[2048,2304]{1,0:T(8,128)(2,1)}, bf16[2048,2304]{1,0:T(8,128)(2,1)}, bf16[2048,896]{1,0:T(8,128)(2,1)}) custom-call(bf16[2048,896]{1,0:T(8,128)(2,1)} %get-tuple-element.28.h, bf16[2048,896]{1,0:T(8,128)(2,1)} %bitcast.50, bf16[896,2304]{1,0:T(8,128)(2,1)} %get-tuple-element.30.wg, ...), custom_call_target="tpu_custom_call" | custom-call | tf_op jit(solution)/shard_map/middle/pallas_call | solution.py:575
  202.4 15.3 %convolution_convert_fusion.4.dd = bf16[2304,896]{1,0:T(8,128)(2,1)} fusion(bf16[2048,2304]{1,0:T(8,128)(2,1)} %get-tuple-element.44, bf16[2048,896]{1,0:T(8,128)(2,1)} %get-tuple-element.33.dh), kind=kOutput, calls=%fused_computation.4 | convolution fusion | flops 8457781248 | bytes 17235968 | tf_op jit(solution)/shard_map/dot_general | solution.py:626
  217.8 10.7 %convolution_convert_fusion.3.dg = bf16[896,2304]{1,0:T(8,128)(2,1)} fusion(bf16[2048,896]{1,0:T(8,128)(2,1)S(1)} %copy-done.4, bf16[2048,2304]{1,0:T(8,128)(2,1)S(1)} %copy-done.2), kind=kOutput, calls=%fused_computation.3 | convolution fusion | flops 8457781248 | bytes 17235968 | tf_op jit(solution)/shard_map/dot_general | solution.py:626
  228.4 0.0 copy-start
  228.5 12.7 %convolution_convert_fusion.2.du = bf16[896,2304]{1,0:T(8,128)(2,1)} fusion(bf16[2048,896]{1,0:T(8,128)(2,1)} %get-tuple-element.36, bf16[2048,2304]{1,0:T(8,128)(2,1)S(1)} %bitcast.55), kind=kOutput, calls=%fused_computation.2 | convolution fusion | flops 8457781248 | bytes 17235968 | tf_op jit(solution)/shard_map/dot_general | solution.py:626
  241.2 12.0 %convolution_convert_fusion.5.dd = bf16[2304,896]{1,0:T(8,128)(2,1)} fusion(bf16[2048,2304]{1,0:T(8,128)(2,1)S(1)} %bitcast.53, bf16[1,2048,896]{2,1,0:T(8,128)(2,1)S(1)} %copy-done), kind=kOutput, calls=%fused_computation.5 | convolution fusion | flops 8457781248 | bytes 17235968 | tf_op jit(solution)/shard_map/dot_general | solution.py:626
  253.2 15.1 %pack.2 = bf16[8,256,3328]{2,1,0:T(8,128)(2,1)} custom-call(bf16[896,2304]{1,0:T(8,128)(2,1)} %convolution_convert_fusion.3.dg, bf16[896,2304]{1,0:T(8,128)(2,1)} %convolution_convert_fusion.2.du, bf16[2304,896]{1,0:T(8,128)(2,1)} %convolution_convert_fusion.5.dd, bf16[224,256]{1,0:T(8,128)(2,1)} %constant.9.clone.gu, bf16[288,256]{1,0:T(8,128)(2,1)} %constant.10.clone.main, ...), custom_call_target="tpu_custom_call" | custom-call | tf_op jit(solution)/shard_map/pack/pallas_call | solution.py:466
  268.3 72.6 %backward.1 = (bf16[2048,2304]{1,0:T(8,128)(2,1)}, bf16[2048,2304]{1,0:T(8,128)(2,1)}, bf16[2048,896]{1,0:T(8,128)(2,1)}, bf16[16,3328]{1,0:T(8,128)(2,1)}) custom-call(bf16[2048,896]{1,0:T(8,128)(2,1)} %bitcast.48, bf16[2048,896]{1,0:T(8,128)(2,1)} %get-tuple-element.33.dh, f32[2048,2304]{1,0:T(8,128)} %get-tuple-element.34.g_in, ...), custom_call_target="tpu_custom_call" | custom-call | tf_op jit(solution)/shard_map/backward/pallas_call | solution.py:613
  340.9 0.7 slice.79
  341.6 0.8 slice.78
  342.4 0.8 slice_bitcast_fusion
  343.2 15.2 %convolution_convert_fusion.1.dg = bf16[896,2304]{1,0:T(8,128)(2,1)} fusion(bf16[2048,896]{1,0:T(8,128)(2,1)} %get-tuple-element.41, bf16[2048,2304]{1,0:T(8,128)(2,1)} %get-tuple-element.42), kind=kOutput, calls=%fused_computation.1 | convolution fusion | flops 8457781248 | bytes 17235968 | tf_op jit(solution)/shard_map/dot_general | solution.py:626
  358.4 10.7 %convolution_convert_fusion.du = bf16[896,2304]{1,0:T(8,128)(2,1)} fusion(bf16[2048,896]{1,0:T(8,128)(2,1)S(1)} %copy-done.3, bf16[2048,2304]{1,0:T(8,128)(2,1)S(1)} %copy-done.1), kind=kOutput, calls=%fused_computation | convolution fusion | flops 8457781248 | bytes 17235968 | tf_op jit(solution)/shard_map/dot_general | solution.py:626
  369.1 15.2 %pack.3 = bf16[8,256,3328]{2,1,0:T(8,128)(2,1)} custom-call(bf16[896,2304]{1,0:T(8,128)(2,1)} %convolution_convert_fusion.1.dg, bf16[896,2304]{1,0:T(8,128)(2,1)} %convolution_convert_fusion.du, bf16[2304,896]{1,0:T(8,128)(2,1)} %convolution_convert_fusion.4.dd, bf16[224,256]{1,0:T(8,128)(2,1)} %constant.9.clone.gu, bf16[288,256]{1,0:T(8,128)(2,1)} %constant.10.clone.main, ...), custom_call_target="tpu_custom_call" | custom-call | tf_op jit(solution)/shard_map/pack/pallas_call | solution.py:466
  384.3 50.1 %scatter.1 = bf16[16,3328]{1,0:T(8,128)(2,1)} custom-call(bf16[4,4,4,2,16,3328]{5,4,3,2,1,0:T(8,128)(2,1)} %bitcast.45), custom_call_target="tpu_custom_call" | custom-call | tf_op jit(solution)/shard_map/scatter/pallas_call | solution.py:370
  434.4 0.7 slice.77
  435.1 0.8 slice.76
  435.9 0.8 slice_bitcast_fusion.1
  436.7 0.7 copy.37
  437.4 0.7 copy.38
  438.1 0.7 copy.36
  438.8 4.2 copy.52
  (35 shorter events, 0.2 us)
Async XLA Ops:
  202.4 15.3 %copy-start.2 = (bf16[2048,2304]{1,0:T(8,128)(2,1)S(1)}, bf16[2048,2304]{1,0:T(8,128)(2,1)}, u32[]{:S(2)}) copy-start(bf16[2048,2304]{1,0:T(8,128)(2,1)} %get-tuple-element.37) | copy-start | bytes 28311556
  202.4 15.3 %copy-start.4 = (bf16[2048,896]{1,0:T(8,128)(2,1)S(1)}, bf16[2048,896]{1,0:T(8,128)(2,1)}, u32[]{:S(2)}) copy-start(bf16[2048,896]{1,0:T(8,128)(2,1)} %get-tuple-element.36) | copy-start | bytes 11010052
  202.4 26.0 %slice-start.3 = ((s8[9437184]{0:T(1024)(128)(4,1)}), s8[4194304]{0:T(1024)(128)(4,1)S(1)}, s32[]{:S(2)}) async-start(s8[9437184]{0:T(1024)(128)(4,1)} %bitcast.54), calls=%async_computation.3 | async-start | bytes 8388608
  202.4 26.0 %slice-start.4 = ((s8[9437184]{0:T(1024)(128)(4,1)}), s8[4194304]{0:T(1024)(128)(4,1)S(1)}, s32[]{:S(2)}) async-start(s8[9437184]{0:T(1024)(128)(4,1)} %bitcast.54), calls=%async_computation.4 | async-start | bytes 8388608
  217.7 10.7 %slice-start.5 = ((s8[9437184]{0:T(1024)(128)(4,1)}), s8[1048576]{0:T(1024)(128)(4,1)S(1)}, s32[]{:S(2)}) async-start(s8[9437184]{0:T(1024)(128)(4,1)} %bitcast.54), calls=%async_computation.5 | async-start | bytes 2097152
  217.7 23.5 %slice-start = ((s8[9437184]{0:T(1024)(128)(4,1)}), s8[4194304]{0:T(1024)(128)(4,1)S(1)}, s32[]{:S(2)}) async-start(s8[9437184]{0:T(1024)(128)(4,1)} %bitcast.52), calls=%async_computation | async-start | bytes 8388608
  217.7 23.4 %slice-start.1 = ((s8[9437184]{0:T(1024)(128)(4,1)}), s8[4194304]{0:T(1024)(128)(4,1)S(1)}, s32[]{:S(2)}) async-start(s8[9437184]{0:T(1024)(128)(4,1)} %bitcast.52), calls=%async_computation.1 | async-start | bytes 8388608
  228.4 12.8 %copy-start = (bf16[1,2048,896]{2,1,0:T(8,128)(2,1)S(1)}, bf16[1,2048,896]{2,1,0:T(8,128)(2,1)}, u32[]{:S(2)}) copy-start(bf16[1,2048,896]{2,1,0:T(8,128)(2,1)} %param.18) | copy-start | bytes 11010052
  228.4 12.7 %slice-start.2 = ((s8[9437184]{0:T(1024)(128)(4,1)}), s8[1048576]{0:T(1024)(128)(4,1)S(1)}, s32[]{:S(2)}) async-start(s8[9437184]{0:T(1024)(128)(4,1)} %bitcast.52), calls=%async_computation.2 | async-start | bytes 2097152
  343.2 15.3 %copy-start.1 = (bf16[2048,2304]{1,0:T(8,128)(2,1)S(1)}, bf16[2048,2304]{1,0:T(8,128)(2,1)}, u32[]{:S(2)}) copy-start(bf16[2048,2304]{1,0:T(8,128)(2,1)} %get-tuple-element.43) | copy-start | bytes 28311556
  343.2 15.2 %copy-start.3 = (bf16[2048,896]{1,0:T(8,128)(2,1)S(1)}, bf16[2048,896]{1,0:T(8,128)(2,1)}, u32[]{:S(2)}) copy-start(bf16[2048,896]{1,0:T(8,128)(2,1)} %get-tuple-element.41) | copy-start | bytes 11010052
